TPU v7x, 512 devices: a 8x2x16 block of a 8x8x16 slice. The times are simulated.
512 devices in a mesh: parts: 2 (over y), slab: 16 (over x, core), pencil: 16 (over z).
Axes of the slice: x: 8, y: 2, z: 16, core: 2. Of those that a mesh axis runs over, the one named last changes fastest.
The devices are a block of a 8x8x16 slice.
Arguments:
- solution: float32 [3, 64, 192, 256], P(None, 'slab', 'pencil', 'parts'), parts along dimension 3, may hold values from -6 to 6
- residual: float32 [3, 64, 192, 256], P(None, 'slab', 'pencil', 'parts'), parts along dimension 3, may hold values from -6 to 6
- direction: float32 [3, 64, 192, 256], P(None, 'slab', 'pencil', 'parts'), parts along dimension 3, may hold values from -18 to 18
- material: int32 [64, 192, 256], P('slab', 'pencil', 'parts'), parts along dimension 2, may hold values from 0 to 1, as said below
- fixed: int32 [64, 192, 256], P('slab', 'pencil', 'parts'), parts along dimension 2, may hold values from 0 to 1, as said below
Outputs:
- next_solution: float32 [3, 64, 192, 256], P(None, 'slab', 'pencil', 'parts'), parts along dimension 3
- next_residual: float32 [3, 64, 192, 256], P(None, 'slab', 'pencil', 'parts'), parts along dimension 3
- next_direction: float32 [3, 64, 192, 256], P(None, 'slab', 'pencil', 'parts'), parts along dimension 3
There are 2 independent parts, one for each index of `parts`. A program takes and returns all parts, laid end to end along the dimension named above; each array names one. Nothing has to cross between parts.
Inputs may be any that keep to these rules, and one draw needn't show every extreme that they name: `material`: a 1 marks a solid voxel. `fixed`: 1 exactly on the first and the last node plane along the first grid dimension and on every node that no solid voxel touches (voxels on the last index of any dimension count as absent).
All inputs are finite; a program needn't handle non-finite values.
Results may differ from a plain program's by a relative error of at most 0.0003.
Values sent between devices are 32-bit elements; how exact they have to be, the bound alone decides.
A program may use at most 64 MiB of HBM per device.

v0:
```python
import functools

import jax
import jax.numpy as jnp
import numpy as np
from jax import lax
from jax.sharding import Mesh
from jax.sharding import PartitionSpec as P

SWEEPS = 4
SLAB_PENCIL = ("slab_0", "slab_1", "pencil")
SLAB = ("slab_0", "slab_1")


POISSON = 0.3
VOID_MODULUS = 0.1
DAMPING = 0.6


def padded_2(shard, sides, width):
    for axis, dim in sides:
        size, length = (lax.axis_size(axis), shard.shape[dim])
        up = [(i, (i + 1) % size) for i in range(size - 1)]
        down = [(j, i) for i, j in up]
        last = lax.slice_in_dim(shard, length - width, length, axis=dim)
        leading = lax.slice_in_dim(shard, 0, width, axis=dim)
        before = lax.ppermute(last, axis, up)
        after = lax.ppermute(leading, axis, down)
        shard = jnp.concatenate([before, shard, after], axis=dim)
    return shard


def passed_along(value, axis, steps):
    count = lax.axis_size(axis)
    leading, last = (max(0, -steps), min(count, count - steps))
    return lax.ppermute(value, axis, [(source, source + steps) for source in range(leading, last)])


def over_axes(shard, axes):
    return functools.reduce(lax.psum, axes, shard)


def corner_shift(corner):
    return (corner % 2, corner // 2 % 2, corner // 4)


def element_matrix(size_x, size_y, size_z):
    lame_first = POISSON / ((1.0 + POISSON) * (1.0 - 2.0 * POISSON))
    shear_mod = 0.5 / (1.0 + POISSON)
    elastic = np.zeros((6, 6))
    elastic[:3, :3] = lame_first
    for entry in range(3):
        elastic[entry, entry] = lame_first + 2.0 * shear_mod
        elastic[entry + 3, entry + 3] = shear_mod
    lengths = (size_x, size_y, size_z)
    points = (0.5 - 0.5 / np.sqrt(3.0), 0.5 + 0.5 / np.sqrt(3.0))
    stiffness = np.zeros((24, 24))
    for point_x in points:
        for point_y in points:
            for point_z in points:
                where_at = (point_x, point_y, point_z)
                gradient = np.zeros((3, 8))
                for corner in range(8):
                    corner_bits = corner_shift(corner)
                    shapes = [
                        where_at[axis_no] if corner_bits[axis_no] else 1.0 - where_at[axis_no]
                        for axis_no in range(3)
                    ]
                    for axis_no in range(3):
                        factor = (1.0 if corner_bits[axis_no] else -1.0) / lengths[axis_no]
                        for second in range(3):
                            if second != axis_no:
                                factor = factor * shapes[second]
                        gradient[axis_no, corner] = factor
                strain = np.zeros((6, 24))
                for corner in range(8):
                    for axis_no in range(3):
                        strain[axis_no, axis_no * 8 + corner] = gradient[axis_no, corner]
                    strain[3, 8 + corner] = gradient[2, corner]
                    strain[3, 16 + corner] = gradient[1, corner]
                    strain[4, corner] = gradient[2, corner]
                    strain[4, 16 + corner] = gradient[0, corner]
                    strain[5, corner] = gradient[1, corner]
                    strain[5, 8 + corner] = gradient[0, corner]
                stiffness = stiffness + strain.T @ elastic @ strain * (
                    size_x * size_y * size_z / 8.0
                )
    return jnp.asarray(stiffness, jnp.float32)


def corner_forces(window, moduli, matrix):
    plane_count, row_count, column_count = moduli.shape
    pieces = []
    for corner in range(8):
        shift_x, shift_y, shift_z = corner_shift(corner)
        piece = window[:, shift_z : shift_z + plane_count, shift_y : shift_y + row_count, :]
        pieces.append(jnp.roll(piece, -shift_x, axis=3))
    values = jnp.stack(pieces, axis=1).reshape(24, plane_count * row_count * column_count)
    forces = jnp.dot(matrix, values, precision=lax.Precision.HIGHEST)
    return forces.reshape(3, 8, plane_count, row_count, column_count) * moduli[None, None]


def node_sums(forces, plane_count, row_count):
    summed = None
    for corner in range(8):
        shift_x, shift_y, shift_z = corner_shift(corner)
        piece = forces[
            ...,
            corner,
            1 - shift_z : 1 - shift_z + plane_count,
            1 - shift_y : 1 - shift_y + row_count,
            :,
        ]
        piece = jnp.roll(piece, shift_x, axis=-1)
        summed = piece if summed is None else summed + piece
    return summed


def diagonal_of(window, free_mask, matrix, plane_count, row_count):
    copies = jnp.broadcast_to(window[None], (8,) + window.shape)
    summed = node_sums(copies, plane_count, row_count)
    scale = jnp.stack([matrix[0, 0], matrix[8, 8], matrix[16, 16]])
    return free_mask[None] * scale[:, None, None, None] * summed[None] + (1.0 - free_mask[None])


def pool_moduli(moduli, first_plane, first_row, plane_total, row_total):
    plane_count, row_count, column_count = moduli.shape
    pooled = moduli.reshape(plane_count // 2, 2, row_count // 2, 2, column_count).mean(axis=(1, 3))
    plane_keep = first_plane + jnp.arange(plane_count // 2, dtype=jnp.int32) < plane_total - 1
    row_keep = first_row + jnp.arange(row_count // 2, dtype=jnp.int32) < row_total - 1
    return (
        pooled
        * plane_keep.astype(pooled.dtype)[:, None, None]
        * row_keep.astype(pooled.dtype)[None, :, None]
    )


def pool_free(free_mask):
    plane_count, row_count, column_count = free_mask.shape
    return free_mask.reshape(plane_count // 2, 2, row_count // 2, 2, column_count).max(axis=(1, 3))


def restrict(vector):
    comps, plane_count, row_count, column_count = vector.shape
    return vector.reshape(comps, plane_count // 2, 2, row_count // 2, 2, column_count).sum(
        axis=(2, 4)
    )


def prolong(vector):
    return jnp.repeat(jnp.repeat(vector, 2, axis=1), 2, axis=2)


def apply_window(padded, vector, level):
    free_mask, window, diagonal, matrix, border = level
    forces = corner_forces(padded, window, matrix)
    return (
        free_mask * node_sums(forces, vector.shape[1], vector.shape[2]) + (1.0 - free_mask) * vector
    )


def operate(vector, level):
    return apply_window(level[4](level[0] * vector), vector, level)


def smooth(estimate, remain, level, final):
    update = DAMPING * remain / level[2]
    estimate = estimate + update
    if not final:
        remain = remain - operate(update, level)
    return (estimate, remain)


def solve_bottom(rhs, level):
    estimate = jnp.zeros_like(rhs)
    remain = rhs
    for sweep in range(SWEEPS):
        estimate, remain = smooth(estimate, remain, level, sweep == SWEEPS - 1)
    return estimate


def halo_fine(vector):
    return padded_2(vector, ((SLAB, 1), ("pencil", 2)), 1)


def halo_middle(vector):
    return padded_2(vector, ((SLAB, 1), ("pencil", 2)), 1)


def halo_bottom(vector):
    return padded_2(vector, ((SLAB, 1), ("pencil", 2)), 1)


def per_device(solution, residual, direction, material, fixed):
    plane_count, row_count, column_count = material.shape
    slab_at = lax.axis_index(SLAB)
    pencil_at = lax.axis_index("pencil")
    total_planes = plane_count * lax.axis_size(SLAB)
    total_rows = row_count * lax.axis_size("pencil")
    plane_index = slab_at * plane_count + jnp.arange(plane_count, dtype=jnp.int32)[:, None, None]
    row_index = pencil_at * row_count + jnp.arange(row_count, dtype=jnp.int32)[None, :, None]
    column_index = jnp.arange(column_count, dtype=jnp.int32)[None, None, :]
    exists = (
        (plane_index < total_planes - 1)
        & (row_index < total_rows - 1)
        & (column_index < column_count - 1)
    )
    moduli = jnp.where(material == 1, 1.0, VOID_MODULUS).astype(jnp.float32) * exists.astype(
        jnp.float32
    )
    below = passed_along(moduli, SLAB, 1)
    taller = jnp.concatenate([below, moduli], axis=0)
    beside = passed_along(taller[:, -4:], "pencil", 1)
    moduli_fine = jnp.concatenate([beside, taller], axis=1)
    moduli_mid = pool_moduli(
        moduli_fine,
        slab_at * (plane_count // 2) - 2,
        pencil_at * (row_count // 2) - 2,
        total_planes // 2,
        total_rows // 2,
    )
    moduli_low = pool_moduli(
        moduli_mid,
        slab_at * (plane_count // 4) - 1,
        pencil_at * (row_count // 4) - 1,
        total_planes // 4,
        total_rows // 4,
    )
    free_fine = (1 - fixed).astype(jnp.float32)
    free_mid = pool_free(free_fine)
    free_low = pool_free(free_mid)
    matrix_fine = element_matrix(1.0, 1.0, 1.0)
    matrix_mid = element_matrix(1.0, 2.0, 2.0)
    matrix_low = element_matrix(1.0, 4.0, 4.0)
    window_fine = moduli_fine[3:, 3:]
    window_mid = moduli_mid[1:, 1:]
    diag_fine = diagonal_of(window_fine, free_fine, matrix_fine, plane_count, row_count)
    diag_mid = diagonal_of(window_mid, free_mid, matrix_mid, plane_count // 2, row_count // 2)
    diag_low = diagonal_of(moduli_low, free_low, matrix_low, plane_count // 4, row_count // 4)
    fine = (free_fine, window_fine, diag_fine, matrix_fine, halo_fine)
    middle = (free_mid, window_mid, diag_mid, matrix_mid, halo_middle)
    bottom = (free_low, moduli_low, diag_low, matrix_low, halo_bottom)
    estimate, remain = smooth(jnp.zeros_like(residual), residual, fine, False)
    estimate, remain = smooth(estimate, remain, fine, False)
    mid_rhs = free_mid * restrict(free_fine * remain)
    mid_est, mid_rem = smooth(jnp.zeros_like(mid_rhs), mid_rhs, middle, False)
    low_rhs = free_low * restrict(free_mid * mid_rem)
    low_est = solve_bottom(low_rhs, bottom)
    lift_mid = free_mid * prolong(low_est)
    mid_est = mid_est + lift_mid
    mid_rem = mid_rem - operate(lift_mid, middle)
    mid_est, mid_rem = smooth(mid_est, mid_rem, middle, True)
    lift_fine = free_fine * prolong(mid_est)
    estimate = estimate + lift_fine
    remain = remain - operate(lift_fine, fine)
    estimate, remain = smooth(estimate, remain, fine, False)
    precond, remain = smooth(estimate, remain, fine, True)
    image_old = operate(direction, fine)
    image_new = operate(precond, fine)
    totals = (
        over_axes(jnp.sum(precond * image_old), SLAB_PENCIL),
        over_axes(jnp.sum(direction * image_old), SLAB_PENCIL),
        over_axes(jnp.sum(precond * image_new), SLAB_PENCIL),
        over_axes(jnp.sum(residual * precond), SLAB_PENCIL),
        over_axes(jnp.sum(residual * direction), SLAB_PENCIL),
    )
    beta_coef = -totals[0] / totals[1]
    next_direction = precond + beta_coef * direction
    image = image_new + beta_coef * image_old
    along = totals[3] + beta_coef * totals[4]
    curvature = totals[2] + 2.0 * beta_coef * totals[0] + beta_coef * beta_coef * totals[1]
    step_size = along / curvature
    next_solution = solution + step_size * next_direction
    next_residual = residual - step_size * image
    return (next_solution, next_residual, next_direction)


def solution(mesh):
    finer = Mesh(
        mesh.devices.reshape(mesh.shape["parts"], 8, 2, mesh.shape["pencil"]),
        ("parts", "slab_0", "slab_1", "pencil"),
    )
    in_specs = (
        P(None, SLAB, "pencil", "parts"),
        P(None, SLAB, "pencil", "parts"),
        P(None, SLAB, "pencil", "parts"),
        P(SLAB, "pencil", "parts"),
        P(SLAB, "pencil", "parts"),
    )
    out_specs = (
        P(None, SLAB, "pencil", "parts"),
        P(None, SLAB, "pencil", "parts"),
        P(None, SLAB, "pencil", "parts"),
    )
    return jax.shard_map(
        per_device, mesh=finer, in_specs=in_specs, out_specs=out_specs, check_vma=False
    )
```

profile of v0, /device:TPU:80, one launch (start us, length us, event | category | flops | bytes accessed | tf_op | source)
XLA Modules:
  0.0 313.6 jit_solution(12793231792767874587)
XLA Ops:
  1.5 1.8 collective-permute-start
  4.1 6.0 %collective-permute-start.1 = (f32[8,4,128]{2,0,1:T(8,128)S(1)}, f32[8,4,128]{2,0,1:T(8,128)S(1)}, u32[]{:S(2)}, u32[]{:S(2)}) collective-permute-start(f32[8,4,128]{2,0,1:T(8,128)S(1)} %fusion.103), channel_id=1, source_target_pairs={{0,1},{1,2},{2,3},{3,4},{4,5},{5,6},{6,7},{7,8},{8,9},{9,10},{10,1... | collective-permute-start | bytes 49160 | tf_op jit(solution)/shard_map/ppermute | solution.py:36
  10.3 1.3 collective-permute-done.1
  12.9 1.3 collective-permute-start.3
  14.2 3.7 %collective-permute-start.2 = (f32[3,1,12,128]{3,2,1,0:T(8,128)S(1)}, f32[3,1,12,128]{3,2,1,0:T(8,128)S(1)}, u32[]{:S(2)}, u32[]{:S(2)}) collective-permute-start(f32[3,1,12,128]{3,2,1,0:T(8,128)S(1)} %get-tuple-element.183), channel_id=1, source_target_pairs={{0,16},{16,32},{32,48},{48,64},{64,80},{80,96},{96,112},{112,128},... | collective-permute-start | bytes 55304 | tf_op jit(solution)/shard_map/ppermute | solution.py:27
  18.7 1.3 collective-permute-start.5
  20.1 6.7 %collective-permute-start.4 = (f32[3,6,1,128]{3,2,1,0:T(1,128)S(1)}, f32[3,6,1,128]{3,2,1,0:T(1,128)S(1)}, u32[]{:S(2)}, u32[]{:S(2)}) collective-permute-start(f32[3,6,1,128]{3,2,1,0:T(1,128)S(1)} %get-tuple-element.160), channel_id=1, source_target_pairs={{0,1},{1,2},{2,3},{3,4},{4,5},{5,6},{6,7},{7,8},{8,9},{9,10},{10,1... | collective-permute-start | bytes 27656 | tf_op jit(solution)/shard_map/ppermute | solution.py:27
  26.9 1.2 collective-permute-done.4
  29.7 2.0 stack.315
  33.3 1.3 collective-permute-start.7
  34.7 5.0 %collective-permute-start.6 = (f32[3,1,12,128]{3,2,1,0:T(8,128)S(1)}, f32[3,1,12,128]{3,2,1,0:T(8,128)S(1)}, u32[]{:S(2)}, u32[]{:S(2)}) collective-permute-start(f32[3,1,12,128]{3,2,1,0:T(8,128)S(1)} %get-tuple-element.181), channel_id=1, source_target_pairs={{0,16},{16,32},{32,48},{48,64},{64,80},{80,96},{96,112},{112,128},... | collective-permute-start | bytes 55304 | tf_op jit(solution)/shard_map/ppermute | solution.py:27
  40.5 1.3 collective-permute-start.9
  41.8 6.7 %collective-permute-start.8 = (f32[3,6,1,128]{3,2,1,0:T(1,128)S(1)}, f32[3,6,1,128]{3,2,1,0:T(1,128)S(1)}, u32[]{:S(2)}, u32[]{:S(2)}) collective-permute-start(f32[3,6,1,128]{3,2,1,0:T(1,128)S(1)} %get-tuple-element.144), channel_id=1, source_target_pairs={{0,1},{1,2},{2,3},{3,4},{4,5},{5,6},{6,7},{7,8},{8,9},{9,10},{10,1... | collective-permute-start | bytes 27656 | tf_op jit(solution)/shard_map/ppermute | solution.py:27
  48.5 1.3 collective-permute-done.8
  51.0 0.8 fusion.234
  53.5 1.3 collective-permute-start.11
  54.8 5.0 %collective-permute-start.10 = (f32[3,1,6,128]{3,1,2,0:T(1,128)S(1)}, f32[3,1,6,128]{3,1,2,0:T(1,128)S(1)}, u32[]{:S(2)}, u32[]{:S(2)}) collective-permute-start(f32[3,1,6,128]{3,1,2,0:T(1,128)S(1)} %get-tuple-element.260), channel_id=1, source_target_pairs={{0,16},{16,32},{32,48},{48,64},{64,80},{80,96},{96,112},{112,128},... | collective-permute-start | bytes 27656 | tf_op jit(solution)/shard_map/ppermute | solution.py:27
  60.6 1.3 collective-permute-start.13
  61.9 7.9 %collective-permute-start.12 = (f32[3,4,1,128]{3,1,2,0:T(4,128)S(1)}, f32[3,4,1,128]{3,1,2,0:T(4,128)S(1)}, u32[]{:S(2)}, u32[]{:S(2)}) collective-permute-start(f32[3,4,1,128]{3,1,2,0:T(4,128)S(1)} %get-tuple-element.214), channel_id=1, source_target_pairs={{0,1},{1,2},{2,3},{3,4},{4,5},{5,6},{6,7},{7,8},{8,9},{9,10},{10,1... | collective-permute-start | bytes 18440 | tf_op jit(solution)/shard_map/ppermute | solution.py:27
  69.9 1.2 collective-permute-done.12
  74.5 1.3 collective-permute-start.15
  75.8 4.9 %collective-permute-start.14 = (f32[3,1,3,128]{3,2,0,1:T(4,128)S(1)}, f32[3,1,3,128]{3,2,0,1:T(4,128)S(1)}, u32[]{:S(2)}, u32[]{:S(2)}) collective-permute-start(f32[3,1,3,128]{3,2,0,1:T(4,128)S(1)} %broadcast_multiply_fusion.6), channel_id=1, source_target_pairs={{0,16},{16,32},{32,48},{48,64},{64,80},{80,96},{96,112},{112,128},... | collective-permute-start | bytes 13832 | tf_op jit(solution)/shard_map/ppermute | solution.py:27
  80.7 0.8 collective-permute-done.14
  81.5 1.3 collective-permute-start.17
  82.8 6.7 %collective-permute-start.16 = (f32[3,3,1,128]{3,2,0,1:T(1,128)S(1)}, f32[3,3,1,128]{3,2,0,1:T(1,128)S(1)}, u32[]{:S(2)}, u32[]{:S(2)}) collective-permute-start(f32[3,3,1,128]{3,2,0,1:T(1,128)S(1)} %get-tuple-element.259), channel_id=1, source_target_pairs={{0,1},{1,2},{2,3},{3,4},{4,5},{5,6},{6,7},{7,8},{8,9},{9,10},{10,1... | collective-permute-start | bytes 13832 | tf_op jit(solution)/shard_map/ppermute | solution.py:27
  89.5 1.3 collective-permute-done.16
  92.8 1.3 collective-permute-start.19
  94.1 4.8 %collective-permute-start.18 = (f32[3,1,3,128]{3,2,0,1:T(4,128)S(1)}, f32[3,1,3,128]{3,2,0,1:T(4,128)S(1)}, u32[]{:S(2)}, u32[]{:S(2)}) collective-permute-start(f32[3,1,3,128]{3,2,0,1:T(4,128)S(1)} %get-tuple-element.45), channel_id=1, source_target_pairs={{0,16},{16,32},{32,48},{48,64},{64,80},{80,96},{96,112},{112,128},... | collective-permute-start | bytes 13832 | tf_op jit(solution)/shard_map/ppermute | solution.py:27
  98.9 0.8 collective-permute-done.18
  99.8 1.3 collective-permute-start.21
  101.1 6.7 %collective-permute-start.20 = (f32[3,3,1,128]{3,2,0,1:T(1,128)S(1)}, f32[3,3,1,128]{3,2,0,1:T(1,128)S(1)}, u32[]{:S(2)}, u32[]{:S(2)}) collective-permute-start(f32[3,3,1,128]{3,2,0,1:T(1,128)S(1)} %get-tuple-element.247), channel_id=1, source_target_pairs={{0,1},{1,2},{2,3},{3,4},{4,5},{5,6},{6,7},{7,8},{8,9},{9,10},{10,1... | collective-permute-start | bytes 13832 | tf_op jit(solution)/shard_map/ppermute | solution.py:27
  107.8 1.3 collective-permute-done.20
  110.4 1.3 collective-permute-start.23
  111.7 5.0 %collective-permute-start.22 = (f32[3,1,3,128]{3,2,0,1:T(4,128)S(1)}, f32[3,1,3,128]{3,2,0,1:T(4,128)S(1)}, u32[]{:S(2)}, u32[]{:S(2)}) collective-permute-start(f32[3,1,3,128]{3,2,0,1:T(4,128)S(1)} %fusion.158), channel_id=1, source_target_pairs={{0,16},{16,32},{32,48},{48,64},{64,80},{80,96},{96,112},{112,128},... | collective-permute-start | bytes 13832 | tf_op jit(solution)/shard_map/ppermute | solution.py:27
  117.3 1.3 collective-permute-start.25
  118.6 6.7 %collective-permute-start.24 = (f32[3,3,1,128]{3,2,0,1:T(1,128)S(1)}, f32[3,3,1,128]{3,2,0,1:T(1,128)S(1)}, u32[]{:S(2)}, u32[]{:S(2)}) collective-permute-start(f32[3,3,1,128]{3,2,0,1:T(1,128)S(1)} %get-tuple-element.235), channel_id=1, source_target_pairs={{0,1},{1,2},{2,3},{3,4},{4,5},{5,6},{6,7},{7,8},{8,9},{9,10},{10,1... | collective-permute-start | bytes 13832 | tf_op jit(solution)/shard_map/ppermute | solution.py:27
  125.3 1.3 collective-permute-done.24
  128.1 1.3 collective-permute-start.27
  129.4 4.8 %collective-permute-start.26 = (f32[3,1,6,128]{3,1,2,0:T(1,128)S(1)}, f32[3,1,6,128]{3,1,2,0:T(1,128)S(1)}, u32[]{:S(2)}, u32[]{:S(2)}) collective-permute-start(f32[3,1,6,128]{3,1,2,0:T(1,128)S(1)} %get-tuple-element.222), channel_id=1, source_target_pairs={{0,16},{16,32},{32,48},{48,64},{64,80},{80,96},{96,112},{112,128},... | collective-permute-start | bytes 27656 | tf_op jit(solution)/shard_map/ppermute | solution.py:27
  134.2 0.8 collective-permute-done.26
  135.1 1.3 collective-permute-start.29
  136.4 7.9 %collective-permute-start.28 = (f32[3,4,1,128]{3,1,2,0:T(4,128)S(1)}, f32[3,4,1,128]{3,1,2,0:T(4,128)S(1)}, u32[]{:S(2)}, u32[]{:S(2)}) collective-permute-start(f32[3,4,1,128]{3,1,2,0:T(4,128)S(1)} %get-tuple-element.210), channel_id=1, source_target_pairs={{0,1},{1,2},{2,3},{3,4},{4,5},{5,6},{6,7},{7,8},{8,9},{9,10},{10,1... | collective-permute-start | bytes 18440 | tf_op jit(solution)/shard_map/ppermute | solution.py:27
  147.6 1.3 collective-permute-start.31
  148.9 4.8 %collective-permute-start.30 = (f32[3,1,12,128]{3,2,1,0:T(8,128)S(1)}, f32[3,1,12,128]{3,2,1,0:T(8,128)S(1)}, u32[]{:S(2)}, u32[]{:S(2)}) collective-permute-start(f32[3,1,12,128]{3,2,1,0:T(8,128)S(1)} %get-tuple-element.167), channel_id=1, source_target_pairs={{0,16},{16,32},{32,48},{48,64},{64,80},{80,96},{96,112},{112,128},... | collective-permute-start | bytes 55304 | tf_op jit(solution)/shard_map/ppermute | solution.py:27
  153.7 1.3 collective-permute-start.39
  155.1 5.7 %collective-permute-start.38 = (f32[3,1,12,128]{3,2,1,0:T(8,128)S(1)}, f32[3,1,12,128]{3,2,1,0:T(8,128)S(1)}, u32[]{:S(2)}, u32[]{:S(2)}) collective-permute-start(f32[3,1,12,128]{3,2,1,0:T(8,128)S(1)} %get-tuple-element.163), channel_id=1, source_target_pairs={{0,16},{16,32},{32,48},{48,64},{64,80},{80,96},{96,112},{112,128},... | collective-permute-start | bytes 55304 | tf_op jit(solution)/shard_map/ppermute | solution.py:27
  160.8 1.3 collective-permute-start.33
  162.2 6.1 %collective-permute-start.32 = (f32[3,6,1,128]{3,2,1,0:T(1,128)S(1)}, f32[3,6,1,128]{3,2,1,0:T(1,128)S(1)}, u32[]{:S(2)}, u32[]{:S(2)}) collective-permute-start(f32[3,6,1,128]{3,2,1,0:T(1,128)S(1)} %get-tuple-element.132), channel_id=1, source_target_pairs={{0,1},{1,2},{2,3},{3,4},{4,5},{5,6},{6,7},{7,8},{8,9},{9,10},{10,1... | collective-permute-start | bytes 27656 | tf_op jit(solution)/shard_map/ppermute | solution.py:27
  168.3 1.3 collective-permute-start.41
  169.6 6.1 %collective-permute-start.40 = (f32[3,6,1,128]{3,2,1,0:T(1,128)S(1)}, f32[3,6,1,128]{3,2,1,0:T(1,128)S(1)}, u32[]{:S(2)}, u32[]{:S(2)}) collective-permute-start(f32[3,6,1,128]{3,2,1,0:T(1,128)S(1)} %get-tuple-element.108), channel_id=1, source_target_pairs={{0,1},{1,2},{2,3},{3,4},{4,5},{5,6},{6,7},{7,8},{8,9},{9,10},{10,1... | collective-permute-start | bytes 27656 | tf_op jit(solution)/shard_map/ppermute | solution.py:27
  176.1 1.0 collective-permute-done.40
  179.8 1.3 collective-permute-start.35
  181.1 3.2 %collective-permute-start.34 = (f32[3,1,12,128]{3,2,1,0:T(8,128)S(1)}, f32[3,1,12,128]{3,2,1,0:T(8,128)S(1)}, u32[]{:S(2)}, u32[]{:S(2)}) collective-permute-start(f32[3,1,12,128]{3,2,1,0:T(8,128)S(1)} %get-tuple-element.165), channel_id=1, source_target_pairs={{0,16},{16,32},{32,48},{48,64},{64,80},{80,96},{96,112},{112,128},... | collective-permute-start | bytes 55304 | tf_op jit(solution)/shard_map/ppermute | solution.py:27
  185.1 1.3 collective-permute-start.37
  186.5 6.1 %collective-permute-start.36 = (f32[3,6,1,128]{3,2,1,0:T(1,128)S(1)}, f32[3,6,1,128]{3,2,1,0:T(1,128)S(1)}, u32[]{:S(2)}, u32[]{:S(2)}) collective-permute-start(f32[3,6,1,128]{3,2,1,0:T(1,128)S(1)} %get-tuple-element.120), channel_id=1, source_target_pairs={{0,1},{1,2},{2,3},{3,4},{4,5},{5,6},{6,7},{7,8},{8,9},{9,10},{10,1... | collective-permute-start | bytes 27656 | tf_op jit(solution)/shard_map/ppermute | solution.py:27
  192.6 1.3 collective-permute-done.36
  196.7 1.3 collective-permute-start.43
  198.0 3.6 %collective-permute-start.42 = (f32[3,1,12,128]{3,2,1,0:T(8,128)S(1)}, f32[3,1,12,128]{3,2,1,0:T(8,128)S(1)}, u32[]{:S(2)}, u32[]{:S(2)}) collective-permute-start(f32[3,1,12,128]{3,2,1,0:T(8,128)S(1)} %get-tuple-element.161), channel_id=1, source_target_pairs={{0,16},{16,32},{32,48},{48,64},{64,80},{80,96},{96,112},{112,128},... | collective-permute-start | bytes 55304 | tf_op jit(solution)/shard_map/ppermute | solution.py:27
  202.4 1.3 collective-permute-start.45
  203.7 6.3 %collective-permute-start.44 = (f32[3,6,1,128]{3,2,1,0:T(1,128)S(1)}, f32[3,6,1,128]{3,2,1,0:T(1,128)S(1)}, u32[]{:S(2)}, u32[]{:S(2)}) collective-permute-start(f32[3,6,1,128]{3,2,1,0:T(1,128)S(1)} %get-tuple-element.96), channel_id=1, source_target_pairs={{0,1},{1,2},{2,3},{3,4},{4,5},{5,6},{6,7},{7,8},{8,9},{9,10},{10,1... | collective-permute-start | bytes 27656 | tf_op jit(solution)/shard_map/ppermute | solution.py:27
  214.2 1.0 multiply_reduce_fusion
  215.2 34.8 %all-reduce.1 = (f32[]{:T(128)}, f32[]{:T(128)}, f32[]{:T(128)}, f32[]{:T(128)}, f32[]{:T(128)}) all-reduce(f32[]{:T(128)} %get-tuple-element.19, f32[]{:T(128)} %get-tuple-element.20, f32[]{:T(128)} %get-tuple-element.21, f32[]{:T(128)} %multiply_reduce_fusion.2, ...), channel_id=1, replica_groups=mesh['parts'=2,'slab_0'=8,'slab_1'=2,'pencil'=16] {'slab_0'}, use_global_device_ids=true, to_apply=%region_14.15 | all-reduce | flops 5 | bytes 40 | tf_op jit(solution)/shard_map/psum | solution.py:40
  250.1 3.1 all-reduce.2
  253.2 53.8 %all-reduce = (f32[]{:T(128)}, f32[]{:T(128)}, f32[]{:T(128)}, f32[]{:T(128)}, f32[]{:T(128)}) all-reduce(f32[]{:T(128)} %get-tuple-element.32, f32[]{:T(128)} %get-tuple-element.33, f32[]{:T(128)} %get-tuple-element.34, f32[]{:T(128)} %get-tuple-element.35, ...), channel_id=1, replica_groups=mesh['parts'=2,'slab_0'=8,'slab_1'=2,'pencil'=16] {'pencil'}, use_global_device_ids=true, to_apply=%region_16.17 | all-reduce | flops 5 | bytes 40 | tf_op jit(solution)/shard_map/psum | solution.py:40
  (385 shorter events, 36.0 us)
Async XLA Ops:
  0.6 0.7 copy-start.7
  1.4 2.0 copy-start.4
  1.5 2.7 collective-permute-start
  4.1 7.4 %collective-permute-start.1 = (f32[8,4,128]{2,0,1:T(8,128)S(1)}, f32[8,4,128]{2,0,1:T(8,128)S(1)}, u32[]{:S(2)}, u32[]{:S(2)}) collective-permute-start(f32[8,4,128]{2,0,1:T(8,128)S(1)} %fusion.103), channel_id=1, source_target_pairs={{0,1},{1,2},{2,3},{3,4},{4,5},{5,6},{6,7},{7,8},{8,9},{9,10},{10,1... | collective-permute-start | bytes 49160 | tf_op jit(solution)/shard_map/ppermute | solution.py:36
  12.0 0.9 copy-start
  12.9 5.1 %collective-permute-start.3 = (f32[3,1,12,128]{3,2,1,0:T(8,128)S(1)}, f32[3,1,12,128]{3,2,1,0:T(8,128)S(1)}, u32[]{:S(2)}, u32[]{:S(2)}) collective-permute-start(f32[3,1,12,128]{3,2,1,0:T(8,128)S(1)} %get-tuple-element.184), channel_id=1, source_target_pairs={{16,0},{32,16},{48,32},{64,48},{80,64},{96,80},{112,96},{128,112},... | collective-permute-start | bytes 55304 | tf_op jit(solution)/shard_map/ppermute | solution.py:28
  14.2 4.5 %collective-permute-start.2 = (f32[3,1,12,128]{3,2,1,0:T(8,128)S(1)}, f32[3,1,12,128]{3,2,1,0:T(8,128)S(1)}, u32[]{:S(2)}, u32[]{:S(2)}) collective-permute-start(f32[3,1,12,128]{3,2,1,0:T(8,128)S(1)} %get-tuple-element.183), channel_id=1, source_target_pairs={{0,16},{16,32},{32,48},{48,64},{64,80},{80,96},{96,112},{112,128},... | collective-permute-start | bytes 55304 | tf_op jit(solution)/shard_map/ppermute | solution.py:27
  18.7 8.1 %collective-permute-start.5 = (f32[3,6,1,128]{3,2,1,0:T(1,128)S(1)}, f32[3,6,1,128]{3,2,1,0:T(1,128)S(1)}, u32[]{:S(2)}, u32[]{:S(2)}) collective-permute-start(f32[3,6,1,128]{3,2,1,0:T(1,128)S(1)} %get-tuple-element.159), channel_id=1, source_target_pairs={{1,0},{2,1},{3,2},{4,3},{5,4},{6,5},{7,6},{8,7},{9,8},{10,9},{11,1... | collective-permute-start | bytes 27656 | tf_op jit(solution)/shard_map/ppermute | solution.py:28
  20.1 8.0 %collective-permute-start.4 = (f32[3,6,1,128]{3,2,1,0:T(1,128)S(1)}, f32[3,6,1,128]{3,2,1,0:T(1,128)S(1)}, u32[]{:S(2)}, u32[]{:S(2)}) collective-permute-start(f32[3,6,1,128]{3,2,1,0:T(1,128)S(1)} %get-tuple-element.160), channel_id=1, source_target_pairs={{0,1},{1,2},{2,3},{3,4},{4,5},{5,6},{6,7},{7,8},{8,9},{9,10},{10,1... | collective-permute-start | bytes 27656 | tf_op jit(solution)/shard_map/ppermute | solution.py:27
  29.7 2.0 copy-start.2
  33.3 6.4 %collective-permute-start.7 = (f32[3,1,12,128]{3,2,1,0:T(8,128)S(1)}, f32[3,1,12,128]{3,2,1,0:T(8,128)S(1)}, u32[]{:S(2)}, u32[]{:S(2)}) collective-permute-start(f32[3,1,12,128]{3,2,1,0:T(8,128)S(1)} %get-tuple-element.182), channel_id=1, source_target_pairs={{16,0},{32,16},{48,32},{64,48},{80,64},{96,80},{112,96},{128,112},... | collective-permute-start | bytes 55304 | tf_op jit(solution)/shard_map/ppermute | solution.py:28
  34.7 5.8 %collective-permute-start.6 = (f32[3,1,12,128]{3,2,1,0:T(8,128)S(1)}, f32[3,1,12,128]{3,2,1,0:T(8,128)S(1)}, u32[]{:S(2)}, u32[]{:S(2)}) collective-permute-start(f32[3,1,12,128]{3,2,1,0:T(8,128)S(1)} %get-tuple-element.181), channel_id=1, source_target_pairs={{0,16},{16,32},{32,48},{48,64},{64,80},{80,96},{96,112},{112,128},... | collective-permute-start | bytes 55304 | tf_op jit(solution)/shard_map/ppermute | solution.py:27
  40.5 8.0 %collective-permute-start.9 = (f32[3,6,1,128]{3,2,1,0:T(1,128)S(1)}, f32[3,6,1,128]{3,2,1,0:T(1,128)S(1)}, u32[]{:S(2)}, u32[]{:S(2)}) collective-permute-start(f32[3,6,1,128]{3,2,1,0:T(1,128)S(1)} %get-tuple-element.143), channel_id=1, source_target_pairs={{1,0},{2,1},{3,2},{4,3},{5,4},{6,5},{7,6},{8,7},{9,8},{10,9},{11,1... | collective-permute-start | bytes 27656 | tf_op jit(solution)/shard_map/ppermute | solution.py:28
  41.8 8.0 %collective-permute-start.8 = (f32[3,6,1,128]{3,2,1,0:T(1,128)S(1)}, f32[3,6,1,128]{3,2,1,0:T(1,128)S(1)}, u32[]{:S(2)}, u32[]{:S(2)}) collective-permute-start(f32[3,6,1,128]{3,2,1,0:T(1,128)S(1)} %get-tuple-element.144), channel_id=1, source_target_pairs={{0,1},{1,2},{2,3},{3,4},{4,5},{5,6},{6,7},{7,8},{8,9},{9,10},{10,1... | collective-permute-start | bytes 27656 | tf_op jit(solution)/shard_map/ppermute | solution.py:27
  52.7 0.7 copy-start.9
  53.5 6.4 %collective-permute-start.11 = (f32[3,1,6,128]{3,1,2,0:T(1,128)S(1)}, f32[3,1,6,128]{3,1,2,0:T(1,128)S(1)}, u32[]{:S(2)}, u32[]{:S(2)}) collective-permute-start(f32[3,1,6,128]{3,1,2,0:T(1,128)S(1)} %get-tuple-element.261), channel_id=1, source_target_pairs={{16,0},{32,16},{48,32},{64,48},{80,64},{96,80},{112,96},{128,112},... | collective-permute-start | bytes 27656 | tf_op jit(solution)/shard_map/ppermute | solution.py:28
  54.8 5.8 %collective-permute-start.10 = (f32[3,1,6,128]{3,1,2,0:T(1,128)S(1)}, f32[3,1,6,128]{3,1,2,0:T(1,128)S(1)}, u32[]{:S(2)}, u32[]{:S(2)}) collective-permute-start(f32[3,1,6,128]{3,1,2,0:T(1,128)S(1)} %get-tuple-element.260), channel_id=1, source_target_pairs={{0,16},{16,32},{32,48},{48,64},{64,80},{80,96},{96,112},{112,128},... | collective-permute-start | bytes 27656 | tf_op jit(solution)/shard_map/ppermute | solution.py:27
  60.6 9.3 %collective-permute-start.13 = (f32[3,4,1,128]{3,1,2,0:T(4,128)S(1)}, f32[3,4,1,128]{3,1,2,0:T(4,128)S(1)}, u32[]{:S(2)}, u32[]{:S(2)}) collective-permute-start(f32[3,4,1,128]{3,1,2,0:T(4,128)S(1)} %get-tuple-element.213), channel_id=1, source_target_pairs={{1,0},{2,1},{3,2},{4,3},{5,4},{6,5},{7,6},{8,7},{9,8},{10,9},{11,1... | collective-permute-start | bytes 18440 | tf_op jit(solution)/shard_map/ppermute | solution.py:28
  61.9 9.2 %collective-permute-start.12 = (f32[3,4,1,128]{3,1,2,0:T(4,128)S(1)}, f32[3,4,1,128]{3,1,2,0:T(4,128)S(1)}, u32[]{:S(2)}, u32[]{:S(2)}) collective-permute-start(f32[3,4,1,128]{3,1,2,0:T(4,128)S(1)} %get-tuple-element.214), channel_id=1, source_target_pairs={{0,1},{1,2},{2,3},{3,4},{4,5},{5,6},{6,7},{7,8},{8,9},{9,10},{10,1... | collective-permute-start | bytes 18440 | tf_op jit(solution)/shard_map/ppermute | solution.py:27
  71.9 0.7 copy-start.6
  73.8 0.7 copy-start.8
  74.5 6.2 %collective-permute-start.15 = (f32[3,1,3,128]{3,2,0,1:T(4,128)S(1)}, f32[3,1,3,128]{3,2,0,1:T(4,128)S(1)}, u32[]{:S(2)}, u32[]{:S(2)}) collective-permute-start(f32[3,1,3,128]{3,2,0,1:T(4,128)S(1)} %broadcast_multiply_fusion.6), channel_id=1, source_target_pairs={{16,0},{32,16},{48,32},{64,48},{80,64},{96,80},{112,96},{128,112},... | collective-permute-start | bytes 13832 | tf_op jit(solution)/shard_map/ppermute | solution.py:28
  75.8 5.7 %collective-permute-start.14 = (f32[3,1,3,128]{3,2,0,1:T(4,128)S(1)}, f32[3,1,3,128]{3,2,0,1:T(4,128)S(1)}, u32[]{:S(2)}, u32[]{:S(2)}) collective-permute-start(f32[3,1,3,128]{3,2,0,1:T(4,128)S(1)} %broadcast_multiply_fusion.6), channel_id=1, source_target_pairs={{0,16},{16,32},{32,48},{48,64},{64,80},{80,96},{96,112},{112,128},... | collective-permute-start | bytes 13832 | tf_op jit(solution)/shard_map/ppermute | solution.py:27
  81.5 8.0 %collective-permute-start.17 = (f32[3,3,1,128]{3,2,0,1:T(1,128)S(1)}, f32[3,3,1,128]{3,2,0,1:T(1,128)S(1)}, u32[]{:S(2)}, u32[]{:S(2)}) collective-permute-start(f32[3,3,1,128]{3,2,0,1:T(1,128)S(1)} %get-tuple-element.258), channel_id=1, source_target_pairs={{1,0},{2,1},{3,2},{4,3},{5,4},{6,5},{7,6},{8,7},{9,8},{10,9},{11,1... | collective-permute-start | bytes 13832 | tf_op jit(solution)/shard_map/ppermute | solution.py:28
  82.8 8.0 %collective-permute-start.16 = (f32[3,3,1,128]{3,2,0,1:T(1,128)S(1)}, f32[3,3,1,128]{3,2,0,1:T(1,128)S(1)}, u32[]{:S(2)}, u32[]{:S(2)}) collective-permute-start(f32[3,3,1,128]{3,2,0,1:T(1,128)S(1)} %get-tuple-element.259), channel_id=1, source_target_pairs={{0,1},{1,2},{2,3},{3,4},{4,5},{5,6},{6,7},{7,8},{8,9},{9,10},{10,1... | collective-permute-start | bytes 13832 | tf_op jit(solution)/shard_map/ppermute | solution.py:27
  91.4 0.7 copy-start.3
  92.8 6.1 %collective-permute-start.19 = (f32[3,1,3,128]{3,2,0,1:T(4,128)S(1)}, f32[3,1,3,128]{3,2,0,1:T(4,128)S(1)}, u32[]{:S(2)}, u32[]{:S(2)}) collective-permute-start(f32[3,1,3,128]{3,2,0,1:T(4,128)S(1)} %get-tuple-element.45), channel_id=1, source_target_pairs={{16,0},{32,16},{48,32},{64,48},{80,64},{96,80},{112,96},{128,112},... | collective-permute-start | bytes 13832 | tf_op jit(solution)/shard_map/ppermute | solution.py:28
  94.1 5.6 %collective-permute-start.18 = (f32[3,1,3,128]{3,2,0,1:T(4,128)S(1)}, f32[3,1,3,128]{3,2,0,1:T(4,128)S(1)}, u32[]{:S(2)}, u32[]{:S(2)}) collective-permute-start(f32[3,1,3,128]{3,2,0,1:T(4,128)S(1)} %get-tuple-element.45), channel_id=1, source_target_pairs={{0,16},{16,32},{32,48},{48,64},{64,80},{80,96},{96,112},{112,128},... | collective-permute-start | bytes 13832 | tf_op jit(solution)/shard_map/ppermute | solution.py:27
  99.8 8.0 %collective-permute-start.21 = (f32[3,3,1,128]{3,2,0,1:T(1,128)S(1)}, f32[3,3,1,128]{3,2,0,1:T(1,128)S(1)}, u32[]{:S(2)}, u32[]{:S(2)}) collective-permute-start(f32[3,3,1,128]{3,2,0,1:T(1,128)S(1)} %get-tuple-element.246), channel_id=1, source_target_pairs={{1,0},{2,1},{3,2},{4,3},{5,4},{6,5},{7,6},{8,7},{9,8},{10,9},{11,1... | collective-permute-start | bytes 13832 | tf_op jit(solution)/shard_map/ppermute | solution.py:28
  101.1 8.0 %collective-permute-start.20 = (f32[3,3,1,128]{3,2,0,1:T(1,128)S(1)}, f32[3,3,1,128]{3,2,0,1:T(1,128)S(1)}, u32[]{:S(2)}, u32[]{:S(2)}) collective-permute-start(f32[3,3,1,128]{3,2,0,1:T(1,128)S(1)} %get-tuple-element.247), channel_id=1, source_target_pairs={{0,1},{1,2},{2,3},{3,4},{4,5},{5,6},{6,7},{7,8},{8,9},{9,10},{10,1... | collective-permute-start | bytes 13832 | tf_op jit(solution)/shard_map/ppermute | solution.py:27
  110.4 6.3 %collective-permute-start.23 = (f32[3,1,3,128]{3,2,0,1:T(4,128)S(1)}, f32[3,1,3,128]{3,2,0,1:T(4,128)S(1)}, u32[]{:S(2)}, u32[]{:S(2)}) collective-permute-start(f32[3,1,3,128]{3,2,0,1:T(4,128)S(1)} %fusion.158), channel_id=1, source_target_pairs={{16,0},{32,16},{48,32},{64,48},{80,64},{96,80},{112,96},{128,112},... | collective-permute-start | bytes 13832 | tf_op jit(solution)/shard_map/ppermute | solution.py:28
  111.7 5.6 %collective-permute-start.22 = (f32[3,1,3,128]{3,2,0,1:T(4,128)S(1)}, f32[3,1,3,128]{3,2,0,1:T(4,128)S(1)}, u32[]{:S(2)}, u32[]{:S(2)}) collective-permute-start(f32[3,1,3,128]{3,2,0,1:T(4,128)S(1)} %fusion.158), channel_id=1, source_target_pairs={{0,16},{16,32},{32,48},{48,64},{64,80},{80,96},{96,112},{112,128},... | collective-permute-start | bytes 13832 | tf_op jit(solution)/shard_map/ppermute | solution.py:27
  117.3 8.0 %collective-permute-start.25 = (f32[3,3,1,128]{3,2,0,1:T(1,128)S(1)}, f32[3,3,1,128]{3,2,0,1:T(1,128)S(1)}, u32[]{:S(2)}, u32[]{:S(2)}) collective-permute-start(f32[3,3,1,128]{3,2,0,1:T(1,128)S(1)} %get-tuple-element.234), channel_id=1, source_target_pairs={{1,0},{2,1},{3,2},{4,3},{5,4},{6,5},{7,6},{8,7},{9,8},{10,9},{11,1... | collective-permute-start | bytes 13832 | tf_op jit(solution)/shard_map/ppermute | solution.py:28
  118.6 8.0 %collective-permute-start.24 = (f32[3,3,1,128]{3,2,0,1:T(1,128)S(1)}, f32[3,3,1,128]{3,2,0,1:T(1,128)S(1)}, u32[]{:S(2)}, u32[]{:S(2)}) collective-permute-start(f32[3,3,1,128]{3,2,0,1:T(1,128)S(1)} %get-tuple-element.235), channel_id=1, source_target_pairs={{0,1},{1,2},{2,3},{3,4},{4,5},{5,6},{6,7},{7,8},{8,9},{9,10},{10,1... | collective-permute-start | bytes 13832 | tf_op jit(solution)/shard_map/ppermute | solution.py:27
  128.0 16.2 %copy-start.1 = (f32[3,4,12,128]{3,1,2,0:T(4,128)S(1)}, f32[3,4,12,128]{3,1,2,0:T(4,128)}, u32[]{:S(2)}) copy-start(f32[3,4,12,128]{3,1,2,0:T(4,128)} %param.10) | copy-start | bytes 221188
  128.1 6.1 %collective-permute-start.27 = (f32[3,1,6,128]{3,1,2,0:T(1,128)S(1)}, f32[3,1,6,128]{3,1,2,0:T(1,128)S(1)}, u32[]{:S(2)}, u32[]{:S(2)}) collective-permute-start(f32[3,1,6,128]{3,1,2,0:T(1,128)S(1)} %get-tuple-element.223), channel_id=1, source_target_pairs={{16,0},{32,16},{48,32},{64,48},{80,64},{96,80},{112,96},{128,112},... | collective-permute-start | bytes 27656 | tf_op jit(solution)/shard_map/ppermute | solution.py:28
  129.4 5.6 %collective-permute-start.26 = (f32[3,1,6,128]{3,1,2,0:T(1,128)S(1)}, f32[3,1,6,128]{3,1,2,0:T(1,128)S(1)}, u32[]{:S(2)}, u32[]{:S(2)}) collective-permute-start(f32[3,1,6,128]{3,1,2,0:T(1,128)S(1)} %get-tuple-element.222), channel_id=1, source_target_pairs={{0,16},{16,32},{32,48},{48,64},{64,80},{80,96},{96,112},{112,128},... | collective-permute-start | bytes 27656 | tf_op jit(solution)/shard_map/ppermute | solution.py:27
  135.1 9.9 %collective-permute-start.29 = (f32[3,4,1,128]{3,1,2,0:T(4,128)S(1)}, f32[3,4,1,128]{3,1,2,0:T(4,128)S(1)}, u32[]{:S(2)}, u32[]{:S(2)}) collective-permute-start(f32[3,4,1,128]{3,1,2,0:T(4,128)S(1)} %get-tuple-element.209), channel_id=1, source_target_pairs={{1,0},{2,1},{3,2},{4,3},{5,4},{6,5},{7,6},{8,7},{9,8},{10,9},{11,1... | collective-permute-start | bytes 18440 | tf_op jit(solution)/shard_map/ppermute | solution.py:28
  136.4 9.2 %collective-permute-start.28 = (f32[3,4,1,128]{3,1,2,0:T(4,128)S(1)}, f32[3,4,1,128]{3,1,2,0:T(4,128)S(1)}, u32[]{:S(2)}, u32[]{:S(2)}) collective-permute-start(f32[3,4,1,128]{3,1,2,0:T(4,128)S(1)} %get-tuple-element.210), channel_id=1, source_target_pairs={{0,1},{1,2},{2,3},{3,4},{4,5},{5,6},{6,7},{7,8},{8,9},{9,10},{10,1... | collective-permute-start | bytes 18440 | tf_op jit(solution)/shard_map/ppermute | solution.py:27
  147.6 13.2 %collective-permute-start.31 = (f32[3,1,12,128]{3,2,1,0:T(8,128)S(1)}, f32[3,1,12,128]{3,2,1,0:T(8,128)S(1)}, u32[]{:S(2)}, u32[]{:S(2)}) collective-permute-start(f32[3,1,12,128]{3,2,1,0:T(8,128)S(1)} %get-tuple-element.168), channel_id=1, source_target_pairs={{16,0},{32,16},{48,32},{64,48},{80,64},{96,80},{112,96},{128,112},... | collective-permute-start | bytes 55304 | tf_op jit(solution)/shard_map/ppermute | solution.py:28
  148.9 11.9 %collective-permute-start.30 = (f32[3,1,12,128]{3,2,1,0:T(8,128)S(1)}, f32[3,1,12,128]{3,2,1,0:T(8,128)S(1)}, u32[]{:S(2)}, u32[]{:S(2)}) collective-permute-start(f32[3,1,12,128]{3,2,1,0:T(8,128)S(1)} %get-tuple-element.167), channel_id=1, source_target_pairs={{0,16},{16,32},{32,48},{48,64},{64,80},{80,96},{96,112},{112,128},... | collective-permute-start | bytes 55304 | tf_op jit(solution)/shard_map/ppermute | solution.py:27
  153.7 14.5 %collective-permute-start.39 = (f32[3,1,12,128]{3,2,1,0:T(8,128)S(1)}, f32[3,1,12,128]{3,2,1,0:T(8,128)S(1)}, u32[]{:S(2)}, u32[]{:S(2)}) collective-permute-start(f32[3,1,12,128]{3,2,1,0:T(8,128)S(1)} %get-tuple-element.164), channel_id=1, source_target_pairs={{16,0},{32,16},{48,32},{64,48},{80,64},{96,80},{112,96},{128,112},... | collective-permute-start | bytes 55304 | tf_op jit(solution)/shard_map/ppermute | solution.py:28
  155.1 13.2 %collective-permute-start.38 = (f32[3,1,12,128]{3,2,1,0:T(8,128)S(1)}, f32[3,1,12,128]{3,2,1,0:T(8,128)S(1)}, u32[]{:S(2)}, u32[]{:S(2)}) collective-permute-start(f32[3,1,12,128]{3,2,1,0:T(8,128)S(1)} %get-tuple-element.163), channel_id=1, source_target_pairs={{0,16},{16,32},{32,48},{48,64},{64,80},{80,96},{96,112},{112,128},... | collective-permute-start | bytes 55304 | tf_op jit(solution)/shard_map/ppermute | solution.py:27
  160.8 14.9 %collective-permute-start.33 = (f32[3,6,1,128]{3,2,1,0:T(1,128)S(1)}, f32[3,6,1,128]{3,2,1,0:T(1,128)S(1)}, u32[]{:S(2)}, u32[]{:S(2)}) collective-permute-start(f32[3,6,1,128]{3,2,1,0:T(1,128)S(1)} %get-tuple-element.131), channel_id=1, source_target_pairs={{1,0},{2,1},{3,2},{4,3},{5,4},{6,5},{7,6},{8,7},{9,8},{10,9},{11,1... | collective-permute-start | bytes 27656 | tf_op jit(solution)/shard_map/ppermute | solution.py:28
  162.2 13.6 %collective-permute-start.32 = (f32[3,6,1,128]{3,2,1,0:T(1,128)S(1)}, f32[3,6,1,128]{3,2,1,0:T(1,128)S(1)}, u32[]{:S(2)}, u32[]{:S(2)}) collective-permute-start(f32[3,6,1,128]{3,2,1,0:T(1,128)S(1)} %get-tuple-element.132), channel_id=1, source_target_pairs={{0,1},{1,2},{2,3},{3,4},{4,5},{5,6},{6,7},{7,8},{8,9},{9,10},{10,1... | collective-permute-start | bytes 27656 | tf_op jit(solution)/shard_map/ppermute | solution.py:27
  168.3 7.8 %collective-permute-start.41 = (f32[3,6,1,128]{3,2,1,0:T(1,128)S(1)}, f32[3,6,1,128]{3,2,1,0:T(1,128)S(1)}, u32[]{:S(2)}, u32[]{:S(2)}) collective-permute-start(f32[3,6,1,128]{3,2,1,0:T(1,128)S(1)} %get-tuple-element.107), channel_id=1, source_target_pairs={{1,0},{2,1},{3,2},{4,3},{5,4},{6,5},{7,6},{8,7},{9,8},{10,9},{11,1... | collective-permute-start | bytes 27656 | tf_op jit(solution)/shard_map/ppermute | solution.py:28
  169.6 7.4 %collective-permute-start.40 = (f32[3,6,1,128]{3,2,1,0:T(1,128)S(1)}, f32[3,6,1,128]{3,2,1,0:T(1,128)S(1)}, u32[]{:S(2)}, u32[]{:S(2)}) collective-permute-start(f32[3,6,1,128]{3,2,1,0:T(1,128)S(1)} %get-tuple-element.108), channel_id=1, source_target_pairs={{0,1},{1,2},{2,3},{3,4},{4,5},{5,6},{6,7},{7,8},{8,9},{9,10},{10,1... | collective-permute-start | bytes 27656 | tf_op jit(solution)/shard_map/ppermute | solution.py:27
  179.8 4.9 %collective-permute-start.35 = (f32[3,1,12,128]{3,2,1,0:T(8,128)S(1)}, f32[3,1,12,128]{3,2,1,0:T(8,128)S(1)}, u32[]{:S(2)}, u32[]{:S(2)}) collective-permute-start(f32[3,1,12,128]{3,2,1,0:T(8,128)S(1)} %get-tuple-element.166), channel_id=1, source_target_pairs={{16,0},{32,16},{48,32},{64,48},{80,64},{96,80},{112,96},{128,112},... | collective-permute-start | bytes 55304 | tf_op jit(solution)/shard_map/ppermute | solution.py:28
  181.1 4.0 %collective-permute-start.34 = (f32[3,1,12,128]{3,2,1,0:T(8,128)S(1)}, f32[3,1,12,128]{3,2,1,0:T(8,128)S(1)}, u32[]{:S(2)}, u32[]{:S(2)}) collective-permute-start(f32[3,1,12,128]{3,2,1,0:T(8,128)S(1)} %get-tuple-element.165), channel_id=1, source_target_pairs={{0,16},{16,32},{32,48},{48,64},{64,80},{80,96},{96,112},{112,128},... | collective-permute-start | bytes 55304 | tf_op jit(solution)/shard_map/ppermute | solution.py:27
  185.1 7.4 %collective-permute-start.37 = (f32[3,6,1,128]{3,2,1,0:T(1,128)S(1)}, f32[3,6,1,128]{3,2,1,0:T(1,128)S(1)}, u32[]{:S(2)}, u32[]{:S(2)}) collective-permute-start(f32[3,6,1,128]{3,2,1,0:T(1,128)S(1)} %get-tuple-element.119), channel_id=1, source_target_pairs={{1,0},{2,1},{3,2},{4,3},{5,4},{6,5},{7,6},{8,7},{9,8},{10,9},{11,1... | collective-permute-start | bytes 27656 | tf_op jit(solution)/shard_map/ppermute | solution.py:28
  186.5 7.4 %collective-permute-start.36 = (f32[3,6,1,128]{3,2,1,0:T(1,128)S(1)}, f32[3,6,1,128]{3,2,1,0:T(1,128)S(1)}, u32[]{:S(2)}, u32[]{:S(2)}) collective-permute-start(f32[3,6,1,128]{3,2,1,0:T(1,128)S(1)} %get-tuple-element.120), channel_id=1, source_target_pairs={{0,1},{1,2},{2,3},{3,4},{4,5},{5,6},{6,7},{7,8},{8,9},{9,10},{10,1... | collective-permute-start | bytes 27656 | tf_op jit(solution)/shard_map/ppermute | solution.py:27
  196.7 5.2 %collective-permute-start.43 = (f32[3,1,12,128]{3,2,1,0:T(8,128)S(1)}, f32[3,1,12,128]{3,2,1,0:T(8,128)S(1)}, u32[]{:S(2)}, u32[]{:S(2)}) collective-permute-start(f32[3,1,12,128]{3,2,1,0:T(8,128)S(1)} %get-tuple-element.162), channel_id=1, source_target_pairs={{16,0},{32,16},{48,32},{64,48},{80,64},{96,80},{112,96},{128,112},... | collective-permute-start | bytes 55304 | tf_op jit(solution)/shard_map/ppermute | solution.py:28
  198.0 4.4 %collective-permute-start.42 = (f32[3,1,12,128]{3,2,1,0:T(8,128)S(1)}, f32[3,1,12,128]{3,2,1,0:T(8,128)S(1)}, u32[]{:S(2)}, u32[]{:S(2)}) collective-permute-start(f32[3,1,12,128]{3,2,1,0:T(8,128)S(1)} %get-tuple-element.161), channel_id=1, source_target_pairs={{0,16},{16,32},{32,48},{48,64},{64,80},{80,96},{96,112},{112,128},... | collective-permute-start | bytes 55304 | tf_op jit(solution)/shard_map/ppermute | solution.py:27
  202.4 8.4 %collective-permute-start.45 = (f32[3,6,1,128]{3,2,1,0:T(1,128)S(1)}, f32[3,6,1,128]{3,2,1,0:T(1,128)S(1)}, u32[]{:S(2)}, u32[]{:S(2)}) collective-permute-start(f32[3,6,1,128]{3,2,1,0:T(1,128)S(1)} %get-tuple-element.95), channel_id=1, source_target_pairs={{1,0},{2,1},{3,2},{4,3},{5,4},{6,5},{7,6},{8,7},{9,8},{10,9},{11,1... | collective-permute-start | bytes 27656 | tf_op jit(solution)/shard_map/ppermute | solution.py:28
  203.7 7.4 %collective-permute-start.44 = (f32[3,6,1,128]{3,2,1,0:T(1,128)S(1)}, f32[3,6,1,128]{3,2,1,0:T(1,128)S(1)}, u32[]{:S(2)}, u32[]{:S(2)}) collective-permute-start(f32[3,6,1,128]{3,2,1,0:T(1,128)S(1)} %get-tuple-element.96), channel_id=1, source_target_pairs={{0,1},{1,2},{2,3},{3,4},{4,5},{5,6},{6,7},{7,8},{8,9},{9,10},{10,1... | collective-permute-start | bytes 27656 | tf_op jit(solution)/shard_map/ppermute | solution.py:27
  214.2 97.3 %copy-start.5 = (f32[3,4,12,128]{3,1,2,0:T(4,128)S(1)}, f32[3,4,12,128]{3,1,2,0:T(4,128)}, u32[]{:S(2)}) copy-start(f32[3,4,12,128]{3,1,2,0:T(4,128)} %param.8) | copy-start | bytes 221188
where the time goes:
time: 315 us; the launch traced here: 314 us
  starting transfers between devices  161 us (51%)
  blocking collectives  91.8 us (29%)
  waiting for transfers between devices  19 us (6%)
  local copies, waits for them, and re-layouts  17.6 us (6%)
  other arithmetic  10.7 us (3%)
  between operations  7.7 us (2%)
  matrix products  6.11 us (2%)
    ppermute x22, starting transfers between devices, padded_2(): before = lax.ppermute(last, axis, up)  124 us
    psum x3, blocking collectives, over_axes(): return functools.reduce(lax.psum, axes, shard)  91.8 us
    ppermute x22, starting transfers between devices, padded_2(): after = lax.ppermute(leading, axis, down)  28.8 us
    ppermute x22, waiting for transfers between devices, padded_2(): before = lax.ppermute(last, axis, up)  17 us
    ppermute x2, starting transfers between devices, passed_along(): lax.ppermute(value, axis, [(source, source + steps) for source in range(l...  7.85 us
    unnamed x65, local copies, waits for them, and re-layouts  6.42 us
  transfers between devices with their start and end apart: 46, of which 21 were waited for; matrix products, arithmetic and copies ran while one was open for 1% of the time, Pallas kernels for 0%

commit v1 on v0

v1 whole, which is shorter than its diff:
```python
import functools

import jax
import jax.numpy as jnp
import numpy as np
from jax import lax
from jax.experimental import pallas as pl
from jax.experimental.pallas import tpu as pltpu
from jax.sharding import PartitionSpec as P

SWEEPS = 4
POISSON = 0.3
VOID_MODULUS = 0.1
DAMPING = 0.6
LAME = POISSON / ((1.0 + POISSON) * (1.0 - 2.0 * POISSON))
SHEAR = 0.5 / (1.0 + POISSON)
LANES = 128
COMPS = range(3)
MESH = pl.DeviceIdType.MESH

PLANES, ROWS = 4, 12
FINE_O, FINE_S = (6, 8), (14, 32)
MID_O, MID_S = (3, 4), (8, 24)
LOW_O, LOW_S = (3, 4), (7, 24)


def diagonal_entries(lengths):
    volume = lengths[0] * lengths[1] * lengths[2]
    entries = []
    for c in COMPS:
        total = 0.0
        for axis in COMPS:
            weight = (LAME + 2.0 * SHEAR) if axis == c else SHEAR
            total += weight / lengths[axis] ** 2 / 9.0
        entries.append(total * volume)
    return entries


def scaled(value, factor):
    return value if factor == 1.0 else value * factor


def element_forces(modes, modulus, lengths):
    volume = lengths[0] * lengths[1] * lengths[2]
    inv = [1.0 / length for length in lengths]

    def key(*axes):
        return tuple(1 if axis in axes else 0 for axis in COMPS)

    out = [dict() for _ in COMPS]
    e_norm = modulus * (volume / 16.0)
    e_pair = modulus * (volume / 48.0)
    e_last = modulus * (volume / 144.0)
    stretch = [scaled(modes[c][key(c)], inv[c]) for c in COMPS]
    trace = (stretch[0] + stretch[1] + stretch[2]) * LAME
    for c in COMPS:
        out[c][key(c)] = scaled(trace + stretch[c] * (2.0 * SHEAR), inv[c]) * e_norm
    for b, t in ((0, 1), (0, 2), (1, 2)):
        glide = (scaled(modes[b][key(t)], inv[t]) + scaled(modes[t][key(b)], inv[b])) * SHEAR
        glide = glide * e_norm
        out[b][key(t)] = scaled(glide, inv[t])
        out[t][key(b)] = scaled(glide, inv[b])
    for b in COMPS:
        c, t = [axis for axis in COMPS if axis != b]
        one, two = modes[c][key(c, b)], modes[t][key(t, b)]
        both = (scaled(one, inv[c]) + scaled(two, inv[t])) * LAME
        for comp, mine in ((c, one), (t, two)):
            own = 2.0 * SHEAR * inv[comp] ** 2 + SHEAR * inv[b] ** 2
            out[comp][key(comp, b)] = (scaled(both, inv[comp]) + mine * own) * e_pair
    for c in COMPS:
        b, t = [axis for axis in COMPS if axis != c]
        mine = modes[c][key(b, t)]
        first = scaled(mine, inv[b]) + scaled(modes[b][key(c, t)], inv[c])
        second = scaled(mine, inv[t]) + scaled(modes[t][key(c, b)], inv[c])
        both = scaled(first, inv[b]) + scaled(second, inv[t])
        out[c][key(b, t)] = both * SHEAR * e_pair
    for c in COMPS:
        total = 0.0
        for axis in COMPS:
            total += ((LAME + 2.0 * SHEAR) if axis == c else SHEAR) * inv[axis] ** 2
        out[c][key(0, 1, 2)] = modes[c][key(0, 1, 2)] * total * e_last
    return out


class Plane:
    def __init__(self, count, shift, factor=1):
        self.count, self.shift, self.factor = count, shift, factor

    def __add__(self, other):
        return Plane(self.count, self.shift + other, self.factor)

    def doubled(self, extra):
        return Plane(self.count, 2 * self.shift + extra, 2 * self.factor)

    def index(self, origin=0):
        return self.count * self.factor + (self.shift + origin)


def place(plane, origin):
    return plane.index(origin) if isinstance(plane, Plane) else plane + origin


def twice(plane, extra):
    return plane.doubled(extra) if isinstance(plane, Plane) else 2 * plane + extra


def over(planes, body):
    lax.fori_loop(0, planes[1] + 1 - planes[0], lambda i, _: (body(Plane(i, planes[0])), 0)[1], 0)


class Level:
    def __init__(self, origin, lengths, split, sums, modulus, inverse, free):
        self.oz, self.oy = origin
        self.lengths = lengths
        self.split, self.sums = split, sums
        self.modulus, self.inverse, self.free = modulus, inverse, free
        entries = diagonal_entries(lengths)
        self.entries = [entries[0]] if lengths[0] == lengths[1] else [entries[0], entries[1]]

    def at(self, plane, row):
        return place(plane, self.oz), pl.ds(row + self.oy, 8)

    def which(self, c):
        return min(c, len(self.entries) - 1)

    def inverse_of(self, c, plane, row):
        p, r = self.at(plane, row)
        return self.inverse[self.which(c), p, r, :]

    def put_split(self, c, plane, row, value):
        p, r = self.at(plane, row)
        after = pltpu.roll(value, LANES - 1, 1)
        self.split[2 * c, p, r, :] = value + after
        self.split[2 * c + 1, p, r, :] = after - value

    def set_diagonal(self, planes, rows):
        def body(plane):
            for row in rows:
                p, r = self.at(plane, row)
                free = self.free[p, r, :]
                total = self.node_total(plane, row)
                for n, entry in enumerate(self.entries):
                    self.inverse[n, p, r, :] = DAMPING / (free * total * entry + (1.0 - free))

        over(planes, body)

    def node_total(self, plane, row):
        total = None
        for dz in (-1, 0):
            for dy in (-1, 0):
                p, r = self.at(plane + dz, row + dy)
                piece = self.modulus[p, r, :]
                total = piece if total is None else total + piece
        return total + pltpu.roll(total, 1, 1)

    def voxels(self, planes, rows):
        def pieces(plane, row):
            found = []
            for cm in range(6):
                p, r = self.at(plane, row)
                near = self.split[cm, p, r, :]
                p, r = self.at(plane, row + 1)
                far = self.split[cm, p, r, :]
                found += [near + far, far - near]
            return found

        for row in rows:

            def body(count, carry, row=row):
                plane = Plane(count, planes[0])
                lower, held = carry
                upper = pieces(plane + 1, row)
                p, r = self.at(plane, row)
                modes = []
                for c in COMPS:
                    mine = {}
                    for m in range(2):
                        for iy in range(2):
                            k = (2 * c + m) * 2 + iy
                            if m + iy > 0:
                                mine[(m, iy, 0)] = lower[k] + upper[k]
                            mine[(m, iy, 1)] = upper[k] - lower[k]
                    modes.append(mine)
                forces = element_forces(modes, self.modulus[p, r, :], self.lengths)
                keep = []
                for c in COMPS:
                    for m in range(2):
                        node = []
                        for iy in range(2):
                            k = (2 * c + m) * 2 + iy
                            diff = forces[c][(m, iy, 1)]
                            if m + iy > 0:
                                same = forces[c][(m, iy, 0)]
                                node.append(held[k] + (same - diff))
                                keep.append(same + diff)
                            else:
                                node.append(held[k] - diff)
                                keep.append(diff)
                        self.sums[(2 * c + m) * 2, p, r, :] = node[0] - node[1]
                        self.sums[(2 * c + m) * 2 + 1, p, r, :] = node[0] + node[1]
                return upper, keep

            zero = [jnp.zeros((8, LANES), jnp.float32)] * 12
            lax.fori_loop(0, planes[1] + 1 - planes[0], body, (pieces(planes[0], row), zero))

    def applied(self, c, plane, row):
        parts = []
        for m in range(2):
            k = (2 * c + m) * 2
            p, r = self.at(plane, row)
            here = self.sums[k, p, r, :]
            p, r = self.at(plane, row - 1)
            parts.append(here + self.sums[k + 1, p, r, :])
        return (parts[0] - parts[1]) + pltpu.roll(parts[0] + parts[1], 1, 1)


def messages():
    found = []
    for oz in (0, -1, 1):
        for oy in (0, -1, 1):
            if (oz, oy) != (0, 0):
                found.append(("wide", oz, oy, ("wide", oy), {0: 192, -1: 72, 1: 64}[oy]))
    for oy in (0, -1, 1):
        found.append(("far", -2, oy, ("far", oy), {0: 24, -1: 16, 1: 8}[oy]))
    for oz in (0, -1, 1):
        for oy in (0, -1, 1):
            if (oz, oy) != (0, 0):
                rows = (8 if oy else 40) if oz else 16
                found.append(("dir", oz, oy, ("dir", oz, oy), rows))
    for oz in (0, -1, 1, -2, 2, -3, 3):
        for oy in (0, -1, 1):
            if (oz, oy) != (0, 0):
                found.append(("fixlow", oz, oy, ("fixlow",), 16))
    for oz in (0, -1, 1, -2, 2, -3, 3):
        for oy in (0, -1, 1):
            if (oz, oy) != (0, 0):
                found.append(("low", oz, oy, ("low",), 16))
    for oz in (0, -1, 1):
        for oy in (0, -1, 1):
            if (oz, oy) != (0, 0):
                found.append(("mid", oz, oy, ("mid", oy), 24 if oy else 72))
    for oz in (0, -1, 1, -2, 2):
        for oy in (0, -1, 1):
            if (oz, oy) != (0, 0):
                each = 16 if oy else 24
                part = {-2: 1, 2: 0}.get(oz)
                found.append(("lift", oz, oy, ("lift", oy, part), each if part is not None else 2 * each))
    return found


def layout():
    sends, receives = {}, {}
    at_send = at_receive = 0
    for oy in (0, -1, 1):
        each = 16 if oy else 24
        sends[("lift", oy, None)] = at_send
        sends[("lift", oy, 0)] = at_send
        sends[("lift", oy, 1)] = at_send + each
        at_send += 2 * each
    for name, oz, oy, key, rows in messages():
        if key not in sends:
            sends[key] = at_send
            at_send += rows
        receives[(name, oz, oy)] = at_receive
        at_receive += rows
    return sends, at_send, receives, at_receive


def kernel(
    slab_count,
    pencil_count,
    solution_ref,
    residual_ref,
    direction_ref,
    material_ref,
    next_solution_ref,
    next_residual_ref,
    next_direction_ref,
    sol_in,
    res_in,
    dir_in,
    mat,
    res,
    dirn,
    s0,
    e0,
    old,
    e_fine,
    f_fine,
    i_fine,
    x_fine,
    b_fine,
    s1,
    u1,
    c1,
    e_mid,
    f_mid,
    i_mid,
    x_mid,
    b_mid,
    s2,
    e_low,
    f_low,
    m_low,
    i_low,
    x_low,
    b_low,
    outbox,
    inbox,
    part_out,
    slab_in,
    line_out,
    pencil_in,
    local_sem,
    send_sem,
    recv_sem,
    sum_send,
    sum_recv,
):
    slab_at, pencil_at = lax.axis_index("slab"), lax.axis_index("pencil")
    sends, _, receives, _ = layout()
    all_messages = messages()
    fine = Level(FINE_O, (1.0, 1.0, 1.0), x_fine, b_fine, e_fine, i_fine, f_fine)
    mid = Level(MID_O, (1.0, 2.0, 2.0), x_mid, b_mid, e_mid, i_mid, f_mid)
    low = Level(LOW_O, (1.0, 4.0, 4.0), x_low, b_low, e_low, i_low, f_low)

    loads = [
        pltpu.make_async_copy(source, target, local_sem.at[n])
        for n, (source, target) in enumerate(
            ((material_ref, mat), (residual_ref, res_in), (direction_ref, dir_in), (solution_ref, sol_in))
        )
    ]
    for load in loads:
        load.start()

    def there(oz, oy):
        z, y = slab_at + oz, pencil_at + oy
        return (z >= 0) & (z < slab_count) & (y >= 0) & (y < pencil_count)

    inbox[...] = jnp.zeros_like(inbox)

    barrier = pltpu.get_barrier_semaphore()
    greeted = jnp.int32(slab_count + pencil_count - 2)

    def greet_slab(k, _):
        pl.semaphore_signal(
            barrier, inc=1, device_id={"slab": lax.rem(slab_at + k, slab_count)}, device_id_type=MESH
        )
        return 0

    def greet_pencil(k, _):
        pl.semaphore_signal(
            barrier, inc=1, device_id={"pencil": lax.rem(pencil_at + k, pencil_count)}, device_id_type=MESH
        )
        return 0

    lax.fori_loop(1, slab_count, greet_slab, 0)
    lax.fori_loop(1, pencil_count, greet_pencil, 0)
    for oz in (-3, -2, -1, 1, 2, 3):
        for oy in (-1, 1):
            near = there(oz, oy)
            greeted = greeted + jnp.where(near, 1, 0)

            @pl.when(near)
            def _(oz=oz, oy=oy):
                pl.semaphore_signal(
                    barrier,
                    inc=1,
                    device_id={"slab": slab_at + oz, "pencil": pencil_at + oy},
                    device_id_type=MESH,
                )

    for ref in (s0, e_fine, x_fine, b_fine, s1, u1, c1, x_mid, b_mid, s2, e_low, f_low, m_low, i_low, x_low, b_low):
        ref[...] = jnp.zeros_like(ref)
    e_mid[...] = jnp.zeros_like(e_mid)
    f_mid[...] = jnp.zeros_like(f_mid)
    i_mid[...] = jnp.zeros_like(i_mid)
    f_fine[...] = jnp.zeros_like(f_fine)
    i_fine[...] = jnp.zeros_like(i_fine)

    def copy_of(number, oz, oy, key, rows):
        name = all_messages[number][0]
        return pltpu.make_async_remote_copy(
            src_ref=outbox.at[pl.ds(sends[key], rows)],
            dst_ref=inbox.at[pl.ds(receives[(name, oz, oy)], rows)],
            send_sem=send_sem.at[number],
            recv_sem=recv_sem.at[number],
            device_id={"slab": slab_at - oz, "pencil": pencil_at - oy},
            device_id_type=MESH,
        )

    def start(*names):
        for number, (name, oz, oy, key, rows) in enumerate(all_messages):
            if name in names:

                @pl.when(there(-oz, -oy))
                def _(number=number, oz=oz, oy=oy, key=key, rows=rows):
                    copy_of(number, oz, oy, key, rows).start()

    def arrive(*names):
        for number, (name, oz, oy, key, rows) in enumerate(all_messages):
            if name in names:

                @pl.when(there(oz, oy))
                def _(number=number, oz=oz, oy=oy, key=key, rows=rows):
                    copy_of(number, oz, oy, key, rows).wait_recv()

    def take(name, oz, oy):
        return receives[(name, oz, oy)]

    def strided(p, first, count):
        return pl.ds(p + PLANES * first, count, stride=PLANES)

    def planes_first(source, target):
        for c in COMPS:
            for p in range(PLANES):
                for first, count in ((0, 8), (8, 4)):
                    target[c, p, pl.ds(first, count), :] = source[c, strided(p, first, count), :]

    loads[0].wait()
    loads[1].wait()
    planes_first(res_in, res)

    taken_rows = {0: (0, 12), -1: (8, 4), 1: (0, 4)}
    voxel_rows = {0: (0, 12), -1: (6, 6), 1: (0, 4)}
    for oy in (0, -1, 1):
        at = sends[("wide", oy)]
        first, count = taken_rows[oy]
        for c in COMPS:
            for p in range(PLANES):
                outbox[pl.ds(at, count), :] = res[c, p, pl.ds(first, count), :]
                at += count
        first, count = voxel_rows[oy]
        for p in range(PLANES):
            outbox[pl.ds(at, count), :] = (mat[strided(p, first, count), :] == 1).astype(jnp.float32)
            at += count
        at = sends[("far", oy)]
        for p in (2, 3):
            outbox[pl.ds(at, count), :] = (mat[strided(p, first, count), :] == 1).astype(jnp.float32)
            at += count

    loads[2].wait()
    planes_first(dir_in, dirn)
    for name, oz, oy, key, rows in all_messages:
        if name == "dir":
            at = sends[key]
            planes = {0: range(PLANES), -1: (3,), 1: (0,)}[oz]
            first, count = {0: (0, 12), -1: (11, 1), 1: (0, 1)}[oy]
            for c in COMPS:
                for p in planes:
                    outbox[pl.ds(at, count), :] = dirn[c, p, pl.ds(first, count), :]
                    at += count

    pl.semaphore_wait(barrier, greeted)
    start("wide", "far")
    start("dir")

    for c in COMPS:
        for p in range(PLANES):
            s0[c, p + FINE_O[0], pl.ds(FINE_O[1], ROWS), :] = res[c, p, pl.ds(0, ROWS), :]
    for p in range(PLANES):
        for first, count in ((0, 8), (8, 4)):
            e_fine[p + FINE_O[0], pl.ds(first + FINE_O[1], count), :] = (mat[strided(p, first, count), :] == 1).astype(
                jnp.float32
            )

    arrive("wide", "far")
    for oz in (0, -1, 1):
        for oy in (0, -1, 1):
            if (oz, oy) == (0, 0):
                continue
            at = receives[("wide", oz, oy)]
            first, count = {0: (0, 12), -1: (-4, 4), 1: (12, 4)}[oy]
            for c in COMPS:
                for p in range(PLANES):
                    s0[c, p + oz * PLANES + FINE_O[0], pl.ds(first + FINE_O[1], count), :] = inbox[pl.ds(at, count), :]
                    at += count
            first, count = {0: (0, 12), -1: (-6, 6), 1: (12, 4)}[oy]
            for p in range(PLANES):
                e_fine[p + oz * PLANES + FINE_O[0], pl.ds(first + FINE_O[1], count), :] = inbox[pl.ds(at, count), :]
                at += count
    for oy in (0, -1, 1):
        at = receives[("far", -2, oy)]
        first, count = {0: (0, 12), -1: (-6, 6), 1: (12, 4)}[oy]
        for p in (-6, -5):
            e_fine[p + FINE_O[0], pl.ds(first + FINE_O[1], count), :] = inbox[pl.ds(at, count), :]
            at += count

    total_planes, total_rows = slab_count * PLANES, pencil_count * ROWS
    row_iota = lax.broadcasted_iota(jnp.int32, (8, LANES), 0)
    lane_iota = lax.broadcasted_iota(jnp.int32, (8, LANES), 1)

    def moduli_body(p):
        plane = slab_at * PLANES + p.index()
        plane_ok = (plane >= 0) & (plane < total_planes - 1)
        for row in (-8, 0, 8):
            ip, ir = fine.at(p, row)
            rows = row_iota + (pencil_at * ROWS + row)
            keep = (rows >= 0) & (rows < total_rows - 1) & (lane_iota < LANES - 1) & plane_ok
            value = jnp.where(e_fine[ip, ir, :] > 0.5, 1.0, VOID_MODULUS)
            e_fine[ip, ir, :] = jnp.where(keep, value, 0.0)

    over((-6, 7), moduli_body)

    def fine_body(p):
        plane = slab_at * PLANES + p.index()
        inside = (plane > 0) & (plane < total_planes - 1)
        for row in (-5, 3, 8):
            ip, ir = fine.at(p, row)
            total = fine.node_total(p, row)
            free = jnp.where((total > 0.9) & inside, 1.0, 0.0)
            f_fine[ip, ir, :] = free
            i_fine[0, ip, ir, :] = DAMPING / (free * total * fine.entries[0] + (1.0 - free))

    over((-5, 7), fine_body)

    def first_update(p):
        for row in (-4, 4, 8):
            ip, ir = fine.at(p, row)
            weight = i_fine[0, ip, ir, :] * f_fine[ip, ir, :]
            for c in COMPS:
                fine.put_split(c, p, row, s0[c, ip, ir, :] * weight)

    over((-4, 7), first_update)

    def halves(ref, c, p, row):
        found = []
        for dp in range(2):
            for dr in range(2):
                r = pl.ds(2 * row + dr + FINE_O[1], 8, stride=2)
                ip = place(twice(p, dp), FINE_O[0])
                found.append(ref[ip, r, :] if c is None else ref[c, ip, r, :])
        return found

    def mid_moduli(p):
        plane_ok = slab_at * (PLANES // 2) + p.index() < total_planes // 2 - 1
        for row in (-3, 0):
            ip, ir = mid.at(p, row)
            a, b, c, d = halves(e_fine, None, p, row)
            rows = row_iota + (pencil_at * (ROWS // 2) + row)
            keep = (rows < total_rows // 2 - 1) & plane_ok
            e_mid[ip, ir, :] = jnp.where(keep, (a + b + c + d) * 0.25, 0.0)

    over((-3, 3), mid_moduli)

    def mid_free(p):
        for row in (-2, 0):
            ip, ir = mid.at(p, row)
            a, b, c, d = halves(f_fine, None, p, row)
            f_mid[ip, ir, :] = jnp.maximum(jnp.maximum(a, b), jnp.maximum(c, d))

    over((-2, 3), mid_free)
    mid.set_diagonal((-2, 3), (-2, 0))

    def mid_pair(ref, c, p, row):
        found = []
        for dp in range(2):
            for dr in range(2):
                r = pl.ds(2 * row + dr + MID_O[1], 8, stride=2)
                ip = place(twice(p, dp), MID_O[0])
                found.append(ref[ip, r, :] if c is None else ref[c, ip, r, :])
        return found

    for p in (-1, 0):
        ip, ir = low.at(p, -1)
        a, b, c, d = mid_pair(e_mid, None, p, -1)
        rows = row_iota + (pencil_at * (ROWS // 4) - 1)
        keep = (rows < total_rows // 4 - 1) & (slab_at * (PLANES // 4) + p < total_planes // 4 - 1) & (row_iota < 4)
        e_low[ip, ir, :] = jnp.where(keep, (a + b + c + d) * 0.25, 0.0)
    a, b, c, d = mid_pair(f_mid, None, 0, 0)
    ip, ir = low.at(0, 0)
    f_low[ip, ir, :] = jnp.where(row_iota < 3, jnp.maximum(jnp.maximum(a, b), jnp.maximum(c, d)), 0.0)
    m_low[ip, ir, :] = jnp.where(row_iota < 3, low.node_total(0, 0), 0.0)
    at = sends[("fixlow",)]
    own_rows = pl.ds(LOW_O[1], 3)
    for n, ref in enumerate((e_low, f_low, m_low)):
        outbox[pl.ds(at + 3 * n, 3), :] = ref[LOW_O[0], own_rows, :]
    start("fixlow")

    fine.voxels((-4, 6), (-4, 4, 12))

    def fine_step(rows, starting):
        def body(p):
            for row in rows:
                ip, ir = fine.at(p, row)
                free = f_fine[ip, ir, :]
                weight = i_fine[0, ip, ir, :]
                for c in COMPS:
                    remain = s0[c, ip, ir, :]
                    update = weight * remain
                    remain = remain - free * fine.applied(c, p, row) - (1.0 - free) * update
                    s0[c, ip, ir, :] = remain
                    if starting:
                        fine.put_split(c, p, row, free * (weight * remain))

        return body

    def estimate_add(starting):
        def body(p):
            for row in (0, 8):
                ip, ir = fine.at(p, row)
                weight = i_fine[0, ip, ir, :]
                for c in COMPS:
                    update = weight * s0[c, ip, ir, :]
                    e0[c, p.index(), pl.ds(row, 8), :] = update if starting else e0[c, p.index(), pl.ds(row, 8), :] + update

        over((0, 3), body)

    estimate_add(True)
    over((-3, 6), fine_step((-3, 5, 13), True))
    estimate_add(False)
    fine.voxels((-3, 5), (-3, 5, 13))
    over((-2, 5), fine_step((-2, 6), False))

    def mid_first(p):
        ip, ir = mid.at(p, -1)
        free = f_mid[ip, ir, :]
        masks = halves(f_fine, None, p, -1)
        for c in COMPS:
            parts = halves(s0, c, p, -1)
            rhs = free * (
                (parts[0] * masks[0] + parts[1] * masks[1]) + (parts[2] * masks[2] + parts[3] * masks[3])
            )
            s1[c, ip, ir, :] = rhs
            update = mid.inverse_of(c, p, -1) * rhs
            u1[c, ip, ir, :] = update
            mid.put_split(c, p, -1, free * update)

    over((-1, 2), mid_first)
    mid.voxels((-1, 1), (-1,))

    def mid_remain(p):
        ip, ir = mid.at(p, 0)
        free = f_mid[ip, ir, :]
        for c in COMPS:
            s1[c, ip, ir, :] = s1[c, ip, ir, :] - free * mid.applied(c, p, 0) - (1.0 - free) * u1[c, ip, ir, :]

    over((0, 1), mid_remain)

    masks = mid_pair(f_mid, None, 0, 0)
    ip, ir = low.at(0, 0)
    free = f_low[ip, ir, :]
    at = sends[("low",)]
    for c in COMPS:
        parts = mid_pair(s1, c, 0, 0)
        rhs = free * ((parts[0] * masks[0] + parts[1] * masks[1]) + (parts[2] * masks[2] + parts[3] * masks[3]))
        rhs = jnp.where(row_iota < 3, rhs, 0.0)
        s2[c, ip, ir, :] = rhs
        outbox[pl.ds(at + 3 * c, 3), :] = rhs[0:3, :]
    start("low")
    mid_rows = {0: (0, 6), -1: (4, 2), 1: (0, 2)}
    for oy in (0, -1, 1):
        at = sends[("mid", oy)]
        first, count = mid_rows[oy]
        for ref in (s1, u1):
            for c in COMPS:
                for p in range(2):
                    outbox[pl.ds(at, count), :] = ref[c, p + MID_O[0], pl.ds(first + MID_O[1], count), :]
                    at += count
    start("mid")

    arrive("dir")
    arrive("fixlow")
    def direction_rows(plane, first, count, c, value):
        ip, ir = plane + FINE_O[0], pl.ds(first + FINE_O[1], count)
        value = value * f_fine[ip, ir, :]
        after = pltpu.roll(value, LANES - 1, 1)
        x_fine[2 * c, ip, ir, :] = value + after
        x_fine[2 * c + 1, ip, ir, :] = after - value

    for oz in (0, -1, 1):
        for oy in (0, -1, 1):
            planes = {0: range(PLANES), -1: (-1,), 1: (PLANES,)}[oz]
            first, count = {0: (0, 12), -1: (-1, 1), 1: (12, 1)}[oy]
            at = None if (oz, oy) == (0, 0) else receives[("dir", oz, oy)]
            for c in COMPS:
                for p in planes:
                    if at is None:
                        direction_rows(p, first, count, c, dirn[c, p, pl.ds(0, ROWS), :])
                    else:
                        direction_rows(p, first, count, c, inbox[pl.ds(at, count), :])
                        at += count
    fine.voxels((-1, 3), (-1, 7))

    def old_image(p):
        for row in (0, 4):
            ip, ir = fine.at(p, row)
            free = f_fine[ip, ir, :]
            for c in COMPS:
                value = dirn[c, p.index(), pl.ds(row, 8), :]
                old[c, p.index(), pl.ds(row, 8), :] = free * fine.applied(c, p, row) + (1.0 - free) * value

    over((0, 3), old_image)

    def low_window(name, refs):
        for oz in (0, -1, 1, -2, 2, -3, 3):
            for oy in (0, -1, 1):
                if (oz, oy) == (0, 0):
                    continue
                at = receives[(name, oz, oy)]
                for n, ref in enumerate(refs):
                    ref[oz + LOW_O[0], pl.ds(3 * oy + LOW_O[1], 3), :] = inbox[pl.ds(at + 3 * n, 3), :]

    low_window("fixlow", (e_low, f_low, m_low))

    def low_inverse(p):
        for row in (-4, 4):
            ip, ir = low.at(p, row)
            free = f_low[ip, ir, :]
            total = m_low[ip, ir, :]
            for n, entry in enumerate(low.entries):
                i_low[n, ip, ir, :] = DAMPING / (free * total * entry + (1.0 - free))

    over((-3, 3), low_inverse)

    arrive("low")
    low_window("low", [s2.at[c] for c in COMPS])

    def low_split(planes, rows):
        def body(p):
            for row in rows:
                ip, ir = low.at(p, row)
                free = f_low[ip, ir, :]
                for c in COMPS:
                    low.put_split(c, p, row, free * (low.inverse_of(c, p, row) * s2[c, ip, ir, :]))

        over(planes, body)

    ip, ir = low.at(0, 0)
    bottom = [low.inverse_of(c, 0, 0) * s2[c, ip, ir, :] for c in COMPS]
    low_split((-3, 3), (-3, 5))
    for depth in (2, 1, 0):
        low.voxels((-1 - depth, depth), (-1 - depth,))

        def low_step(p, depth=depth):
            row = -depth
            ip, ir = low.at(p, row)
            free = f_low[ip, ir, :]
            for c in COMPS:
                remain = s2[c, ip, ir, :]
                update = low.inverse_of(c, p, row) * remain
                remain = remain - free * low.applied(c, p, row) - (1.0 - free) * update
                s2[c, ip, ir, :] = remain
                if depth:
                    low.put_split(c, p, row, free * (low.inverse_of(c, p, row) * remain))

        over((-depth, depth), low_step)
        ip, ir = low.at(0, 0)
        for c in COMPS:
            bottom[c] = bottom[c] + low.inverse_of(c, 0, 0) * s2[c, ip, ir, :]

    for c in COMPS:
        for p in range(2):
            for dr in range(2):
                c1[c, p + MID_O[0], pl.ds(MID_O[1] + dr, 3, stride=2), :] = bottom[c][0:3, :]
    for c in COMPS:
        for p in range(2):
            ip, ir = p + MID_O[0], pl.ds(MID_O[1], 6)
            c1[c, ip, ir, :] = c1[c, ip, ir, :] * f_mid[ip, ir, :]
    for oy in (0, -1, 1):
        first, count = {0: (0, 6), -1: (3, 3), 1: (0, 3)}[oy]
        for p in range(2):
            at = sends[("lift", oy, p)]
            for c in COMPS:
                outbox[pl.ds(at, count), :] = c1[c, p + MID_O[0], pl.ds(first + MID_O[1], count), :]
                at += count
    start("lift")
    arrive("mid")
    for oz in (0, -1, 1):
        for oy in (0, -1, 1):
            if (oz, oy) == (0, 0):
                continue
            at = receives[("mid", oz, oy)]
            first, count = {0: (0, 6), -1: (-2, 2), 1: (6, 2)}[oy]
            for ref in (s1, u1):
                for c in COMPS:
                    for p in range(2):
                        ref[c, p + 2 * oz + MID_O[0], pl.ds(first + MID_O[1], count), :] = inbox[pl.ds(at, count), :]
                        at += count
    arrive("lift")
    for oz in (0, -1, 1, -2, 2):
        for oy in (0, -1, 1):
            if (oz, oy) == (0, 0):
                continue
            base = receives[("lift", oz, oy)]
            first, count = {0: (0, 6), -1: (-3, 3), 1: (6, 3)}[oy]
            planes = {-2: (-3,), 2: (4,)}.get(oz, (2 * oz, 2 * oz + 1))
            for n, p in enumerate(planes):
                at = base + n * (16 if oy else 24)
                for c in COMPS:
                    c1[c, p + MID_O[0], pl.ds(first + MID_O[1], count), :] = inbox[pl.ds(at, count), :]
                    at += count

    def lift_split(p):
        for row in (-3, 5):
            ip, ir = mid.at(p, row)
            for c in COMPS:
                mid.put_split(c, p, row, c1[c, ip, ir, :])

    over((-3, 4), lift_split)
    mid.voxels((-3, 3), (-3, 5))

    def mid_second(p):
        for row in (-2, 6):
            ip, ir = mid.at(p, row)
            free = f_mid[ip, ir, :]
            for c in COMPS:
                remain = s1[c, ip, ir, :] - free * mid.applied(c, p, row)
                u1[c, ip, ir, :] = u1[c, ip, ir, :] + c1[c, ip, ir, :] + mid.inverse_of(c, p, row) * remain

    over((-2, 3), mid_second)

    def lift_fine(p):
        for row in (-2, 0):
            ip, ir = mid.at(p, row)
            for c in COMPS:
                value = u1[c, ip, ir, :]
                for dp in range(2):
                    for dr in range(2):
                        out = pl.ds(2 * row + dr + FINE_O[1], 8, stride=2)
                        x_fine[2 * c, place(twice(p, dp), FINE_O[0]), out, :] = value

    over((-2, 3), lift_fine)

    def lift_parts(p):
        for row in (-4, 4, 12):
            ip, ir = fine.at(p, row)
            free = f_fine[ip, ir, :]
            for c in COMPS:
                fine.put_split(c, p, row, free * x_fine[2 * c, ip, ir, :])

    def lift_own(p):
        for row in (0, 4):
            ip, ir = fine.at(p, row)
            free = f_fine[ip, ir, :]
            for c in COMPS:
                part = free * x_fine[2 * c, ip, ir, :]
                if row:
                    part = jnp.where(row_iota >= 4, part, 0.0)
                e0[c, p.index(), pl.ds(row, 8), :] = e0[c, p.index(), pl.ds(row, 8), :] + part

    over((0, 3), lift_own)
    over((-4, 7), lift_parts)
    fine.voxels((-3, 5), (-3, 5, 13))

    def lift_step(p):
        for row in (-2, 6):
            ip, ir = fine.at(p, row)
            free = f_fine[ip, ir, :]
            weight = i_fine[0, ip, ir, :]
            for c in COMPS:
                remain = s0[c, ip, ir, :] - free * fine.applied(c, p, row)
                s0[c, ip, ir, :] = remain
                fine.put_split(c, p, row, free * (weight * remain))

    over((-2, 5), lift_step)
    estimate_add(False)
    fine.voxels((-2, 4), (-2, 6))
    over((-1, 4), fine_step((-1, 7), True))
    estimate_add(False)
    fine.voxels((-1, 3), (-1, 7))
    over((0, 3), fine_step((0, 8), False))

    def dots(p, totals):
        totals = list(totals)
        for row in (0, 4):
            ip, ir = p + FINE_O[0], pl.ds(row + FINE_O[1], 8)
            keep = None if row == 0 else row_iota >= 4
            for c in COMPS:
                rows = pl.ds(row, 8)
                z, d, o, r = e0[c, p, rows, :], dirn[c, p, rows, :], old[c, p, rows, :], res[c, p, rows, :]
                new = r - s0[c, ip, ir, :]
                for n, term in enumerate((z * o, d * o, z * new, r * z, r * d)):
                    totals[n] = totals[n] + (term if keep is None else jnp.where(keep, term, 0.0))
        return tuple(totals)

    totals = lax.fori_loop(0, PLANES, dots, (jnp.zeros((8, LANES), jnp.float32),) * 5)
    for n, total in enumerate(totals):
        part_out[pl.ds(n, 1), :] = jnp.sum(total, axis=0, keepdims=True)

    def share(axis, at, count, source, target, which):
        def copy(k):
            return pltpu.make_async_remote_copy(
                src_ref=source,
                dst_ref=target.at[k],
                send_sem=sum_send.at[which, k],
                recv_sem=sum_recv.at[which, k],
                device_id={axis: lax.rem(at + k, count)},
                device_id_type=MESH,
            )

        lax.fori_loop(1, count, lambda k, _: (copy(k).start(), 0)[1], 0)
        lax.fori_loop(1, count, lambda k, _: (copy(k).wait_recv(), 0)[1], 0)
        total = source[...]
        total = lax.fori_loop(1, count, lambda k, t: t + target[k], total)
        return total, copy

    line, slab_copy = share("slab", slab_at, slab_count, part_out, slab_in, 0)
    line_out[...] = line
    whole, pencil_copy = share("pencil", pencil_at, pencil_count, line_out, pencil_in, 1)
    summed = jnp.sum(whole, axis=1, keepdims=True)
    t = [summed[n : n + 1, :] for n in range(5)]
    beta = -t[0] / t[1]
    along = t[3] + beta * t[4]
    curvature = t[2] + 2.0 * beta * t[0] + beta * beta * t[1]
    step = along / curvature

    loads[3].wait()

    for c in COMPS:
        for p in range(PLANES):
            for first, count in ((0, 8), (8, 4)):
                rows, there_rows = pl.ds(first, count), strided(p, first, count)
                z, d, o, r = e0[c, p, rows, :], dirn[c, p, rows, :], old[c, p, rows, :], res[c, p, rows, :]
                new = r - s0[c, p + FINE_O[0], pl.ds(first + FINE_O[1], count), :]
                nd = z + beta * d
                image = new + beta * o
                dir_in[c, there_rows, :] = nd
                sol_in[c, there_rows, :] = sol_in[c, there_rows, :] + step * nd
                res_in[c, there_rows, :] = r - step * image
    stores = [
        pltpu.make_async_copy(source, target, local_sem.at[n])
        for n, (source, target) in enumerate(
            ((dir_in, next_direction_ref), (sol_in, next_solution_ref), (res_in, next_residual_ref))
        )
    ]
    for store in stores:
        store.start()

    for number, (name, oz, oy, key, rows) in enumerate(all_messages):

        @pl.when(there(-oz, -oy))
        def _(number=number, oz=oz, oy=oy, key=key, rows=rows):
            copy_of(number, oz, oy, key, rows).wait_send()

    lax.fori_loop(1, slab_count, lambda k, _: (slab_copy(k).wait_send(), 0)[1], 0)
    lax.fori_loop(1, pencil_count, lambda k, _: (pencil_copy(k).wait_send(), 0)[1], 0)
    for store in stores:
        store.wait()


def per_device(slab_count, pencil_count, solution, residual, direction, material, fixed):
    del fixed
    _, send_rows, _, receive_rows = layout()
    count = len(messages())
    f32 = jnp.float32
    flat = (3, ROWS * PLANES, LANES)
    padded = (3, PLANES, 16, LANES)

    def vmem(*shape):
        return pltpu.VMEM(shape, f32)

    def window(size):
        planes, rows = size
        return planes, rows, LANES

    hbm = pl.BlockSpec(memory_space=pl.ANY)
    out = jax.ShapeDtypeStruct(flat, f32)
    results = pl.pallas_call(
        functools.partial(kernel, slab_count, pencil_count),
        out_shape=(out, out, out),
        in_specs=[hbm] * 4,
        out_specs=(hbm, hbm, hbm),
        scratch_shapes=[
            vmem(*flat),
            vmem(*flat),
            vmem(*flat),
            pltpu.VMEM(flat[1:], jnp.int32),
            vmem(*padded),
            vmem(*padded),
            vmem(3, *window(FINE_S)),
            vmem(*padded),
            vmem(*padded),
            vmem(*window(FINE_S)),
            vmem(*window(FINE_S)),
            vmem(1, *window(FINE_S)),
            vmem(6, *window(FINE_S)),
            vmem(12, *window(FINE_S)),
            vmem(3, *window(MID_S)),
            vmem(3, *window(MID_S)),
            vmem(3, *window(MID_S)),
            vmem(*window(MID_S)),
            vmem(*window(MID_S)),
            vmem(2, *window(MID_S)),
            vmem(6, *window(MID_S)),
            vmem(12, *window(MID_S)),
            vmem(3, *window(LOW_S)),
            vmem(*window(LOW_S)),
            vmem(*window(LOW_S)),
            vmem(*window(LOW_S)),
            vmem(2, *window(LOW_S)),
            vmem(6, *window(LOW_S)),
            vmem(12, *window(LOW_S)),
            vmem(send_rows, LANES),
            vmem(receive_rows, LANES),
            vmem(8, LANES),
            vmem(slab_count, 8, LANES),
            vmem(8, LANES),
            vmem(pencil_count, 8, LANES),
            pltpu.SemaphoreType.DMA((4,)),
            pltpu.SemaphoreType.DMA((count,)),
            pltpu.SemaphoreType.DMA((count,)),
            pltpu.SemaphoreType.DMA((2, max(slab_count, pencil_count))),
            pltpu.SemaphoreType.DMA((2, max(slab_count, pencil_count))),
        ],
        compiler_params=pltpu.CompilerParams(collective_id=0, has_side_effects=True),
    )(*(inward(field) for field in (solution, residual, direction, material)))
    return tuple(outward(field) for field in results)


def inward(field):
    axes = (0, 2, 1, 3) if field.ndim == 4 else (1, 0, 2)
    return field.transpose(axes).reshape(field.shape[:-3] + (ROWS * PLANES, LANES))


def outward(field):
    return field.reshape(3, ROWS, PLANES, LANES).transpose(0, 2, 1, 3)


def solution(mesh):
    field = P(None, "slab", "pencil", "parts")
    mask = P("slab", "pencil", "parts")
    return jax.shard_map(
        functools.partial(per_device, mesh.shape["slab"], mesh.shape["pencil"]),
        mesh=mesh,
        in_specs=(field, field, field, mask, mask),
        out_specs=(field, field, field),
        check_vma=False,
    )
```

time: 315 us -> 103 us (0.33)
  starting transfers between devices: 161 us -> 0 us
  Pallas kernels: 0 us -> 99.1 us
  blocking collectives: 91.8 us -> 0 us
  waiting for transfers between devices: 19 us -> 0 us
  local copies, waits for them, and re-layouts: 17.6 us -> 3.1 us
  other arithmetic: 10.7 us -> 0 us
  between operations: 7.7 us -> 0.65 us
  matrix products: 6.11 us -> 0 us
    ppermute x46 -> x0, starting transfers between devices: 161 us -> none  [the longest x22 124 us: padded_2(): before = lax.ppermute(last, axis, up)]
    pallas_call x0 -> x1, Pallas kernels: none -> 99.1 us  [per_device(): pl.pallas_call(functools.partial(kernel, slab_count, pencil_count), out_s...]
    psum x3 -> x0, blocking collectives: 91.8 us -> none  [over_axes(): return functools.reduce(lax.psum, axes, shard)]
    ppermute x46 -> x0, waiting for transfers between devices: 19 us -> none  [the longest x22 17 us: padded_2(): before = lax.ppermute(last, axis, up)]
    dot_general x11 -> x0, matrix products: 6.11 us -> none  [corner_forces(): forces = jnp.dot(matrix, values, precision=lax.Precision.HIGHEST)]
    slice x90 -> x0, local copies, waits for them, and re-layouts: 5.67 us -> none  [the longest x37 3 us: node_sums(): piece = jnp.roll(piece, shift_x, axis=-1)]
    another operation x20 -> x0, local copies, waits for them, and re-layouts: 4.24 us -> none  [corner_forces(): jnp.stack(pieces, axis=1)]
    unnamed x65 -> x7, local copies, waits for them, and re-layouts: 6.42 us -> 3.1 us
  transfers between devices with their start and end apart: 46 -> 0, of which waited for: 21 -> 0; matrix products, arithmetic and copies ran while one was open for 1% -> 0% of each run, Pallas kernels for 0% -> 0%
where the time goes in v1:
time: 103 us
  Pallas kernels  99.1 us (96%)
  local copies, waits for them, and re-layouts  3.1 us (3%)
    pallas_call x1, Pallas kernels, per_device(): pl.pallas_call(functools.partial(kernel, slab_count, pencil_count), out_s...  99.1 us
    unnamed x7, local copies, waits for them, and re-layouts  3.1 us

profile of v1, /device:TPU:80, one launch (start us, length us, event | category | flops | bytes accessed | tf_op | source)
XLA Modules:
  0.0 102.9 jit_solution(13415905388789493741)
XLA Ops:
  0.6 99.1 %shard_map.67 = (f32[3,48,128]{2,1,0:T(8,128)}, f32[3,48,128]{2,1,0:T(8,128)}, f32[3,48,128]{2,1,0:T(8,128)}) custom-call(f32[3,48,128]{2,1,0:T(8,128)} %bitcast.24, f32[3,48,128]{2,1,0:T(8,128)} %bitcast.25, f32[3,48,128]{2,1,0:T(8,128)} %bitcast.26, s32[48,128]{1,0:T(8,128)} %bitcast.27), custom_call_target="tpu_custom_call" | custom-call | tf_op jit(solution)/shard_map/pallas_call | solution.py:959
  99.7 0.0 copy-start.1
  99.8 1.6 %copy.10 = f32[3,4,12,128]{3,1,2,0:T(4,128)} copy(f32[3,4,12,128]{3,1,2,0:T(4,128)} %bitcast.23) | data formatting | bytes 147456
  101.3 0.0 copy-done.1
  101.3 0.0 copy-start
  101.3 0.6 copy.11
  101.9 0.3 copy-done
  102.2 0.6 copy.12
Async XLA Ops:
  99.7 1.6 %copy-start.1 = (f32[3,48,128]{2,1,0:T(8,128)S(1)}, f32[3,48,128]{2,1,0:T(8,128)}, u32[]{:S(2)}) copy-start(f32[3,48,128]{2,1,0:T(8,128)} %get-tuple-element.7) | copy-start | bytes 221188
  101.3 0.9 copy-start

commit v2 on v1

--- a/solution.py
+++ b/solution.py
@@ -19,6 +19,7 @@
 MESH = pl.DeviceIdType.MESH
 
 PLANES, ROWS = 4, 12
+REACH, STAGES = 3, 6
 FINE_O, FINE_S = (6, 8), (14, 32)
 MID_O, MID_S = (3, 4), (8, 24)
 LOW_O, LOW_S = (3, 4), (7, 24)
@@ -104,8 +105,27 @@
     return plane.doubled(extra) if isinstance(plane, Plane) else 2 * plane + extra
 
 
-def over(planes, body):
-    lax.fori_loop(0, planes[1] + 1 - planes[0], lambda i, _: (body(Plane(i, planes[0])), 0)[1], 0)
+def over(planes, body, group=14):
+    count = planes[1] + 1 - planes[0]
+    group = max(n for n in range(1, group + 1) if count % n == 0)
+
+    def step(i, _):
+        stores = []
+        for n in range(group):
+            stores += body(Plane(i * group if group > 1 else i, planes[0] + n))
+        for ref, index, value in stores:
+            ref[index] = value
+        return 0
+
+    if group == count:
+        stores = [store for n in range(count) for store in body(planes[0] + n)]
+        for ref, index, value in stores:
+            ref[index] = value
+    else:
+        lax.fori_loop(0, count // group, step, 0)
+
+
+ALL = slice(None)
 
 
 class Level:
@@ -130,17 +150,22 @@
     def put_split(self, c, plane, row, value):
         p, r = self.at(plane, row)
         after = pltpu.roll(value, LANES - 1, 1)
-        self.split[2 * c, p, r, :] = value + after
-        self.split[2 * c + 1, p, r, :] = after - value
+        return [
+            (self.split, (2 * c, p, r, ALL), value + after),
+            (self.split, (2 * c + 1, p, r, ALL), after - value),
+        ]
 
     def set_diagonal(self, planes, rows):
         def body(plane):
+            stores = []
             for row in rows:
                 p, r = self.at(plane, row)
                 free = self.free[p, r, :]
                 total = self.node_total(plane, row)
                 for n, entry in enumerate(self.entries):
-                    self.inverse[n, p, r, :] = DAMPING / (free * total * entry + (1.0 - free))
+                    value = DAMPING / (free * total * entry + (1.0 - free))
+                    stores.append((self.inverse, (n, p, r, ALL), value))
+            return stores
 
         over(planes, body)
 
@@ -316,6 +341,7 @@
     recv_sem,
     sum_send,
     sum_recv,
+    word_sem,
 ):
     slab_at, pencil_at = lax.axis_index("slab"), lax.axis_index("pencil")
     sends, _, receives, _ = layout()
@@ -340,35 +366,57 @@
     inbox[...] = jnp.zeros_like(inbox)
 
     barrier = pltpu.get_barrier_semaphore()
-    greeted = jnp.int32(slab_count + pencil_count - 2)
-
-    def greet_slab(k, _):
-        pl.semaphore_signal(
-            barrier, inc=1, device_id={"slab": lax.rem(slab_at + k, slab_count)}, device_id_type=MESH
-        )
-        return 0
-
-    def greet_pencil(k, _):
-        pl.semaphore_signal(
-            barrier, inc=1, device_id={"pencil": lax.rem(pencil_at + k, pencil_count)}, device_id_type=MESH
-        )
-        return 0
-
-    lax.fori_loop(1, slab_count, greet_slab, 0)
-    lax.fori_loop(1, pencil_count, greet_pencil, 0)
-    for oz in (-3, -2, -1, 1, 2, 3):
-        for oy in (-1, 1):
-            near = there(oz, oy)
-            greeted = greeted + jnp.where(near, 1, 0)
-
-            @pl.when(near)
-            def _(oz=oz, oy=oy):
-                pl.semaphore_signal(
-                    barrier,
-                    inc=1,
-                    device_id={"slab": slab_at + oz, "pencil": pencil_at + oy},
-                    device_id_type=MESH,
-                )
+    greeted = jnp.int32(0)
+    for oz in range(-REACH, REACH + 1):
+        for oy in (-1, 0, 1):
+            if (oz, oy) != (0, 0):
+                near = there(oz, oy)
+                greeted = greeted + jnp.where(near, 1, 0)
+
+                @pl.when(near)
+                def _(oz=oz, oy=oy):
+                    pl.semaphore_signal(
+                        barrier,
+                        inc=1,
+                        device_id={"slab": slab_at + oz, "pencil": pencil_at + oy},
+                        device_id_type=MESH,
+                    )
+
+    def stages(count, known):
+        steps = []
+        while known < count - 1:
+            step = min(known, count - 1 - known)
+            steps.append(step)
+            known += step
+        return steps
+
+    plan = [("slab", stages(slab_count, REACH)), ("pencil", stages(pencil_count, 1))]
+
+    def sides(axis, step):
+        return [(step * sign if axis == "slab" else 0, step * sign if axis == "pencil" else 0) for sign in (-1, 1)]
+
+    def tell(stage):
+        for which, (axis, steps) in enumerate(plan):
+            if stage < len(steps):
+                for side, (oz, oy) in enumerate(sides(axis, steps[stage])):
+
+                    @pl.when(there(oz, oy))
+                    def _(oz=oz, oy=oy):
+                        pl.semaphore_signal(
+                            word_sem.at[which, stage, 1 - side],
+                            inc=1,
+                            device_id={"slab": slab_at + oz, "pencil": pencil_at + oy},
+                            device_id_type=MESH,
+                        )
+
+    def hear(stage):
+        for which, (axis, steps) in enumerate(plan):
+            if stage < len(steps):
+                for side, (oz, oy) in enumerate(sides(axis, steps[stage])):
+
+                    @pl.when(there(oz, oy))
+                    def _():
+                        pl.semaphore_wait(word_sem.at[which, stage, side], 1)
 
     for ref in (s0, e_fine, x_fine, b_fine, s1, u1, c1, x_mid, b_mid, s2, e_low, f_low, m_low, i_low, x_low, b_low):
         ref[...] = jnp.zeros_like(ref)
@@ -454,6 +502,7 @@
     pl.semaphore_wait(barrier, greeted)
     start("wide", "far")
     start("dir")
+    tell(0)
 
     for c in COMPS:
         for p in range(PLANES):
@@ -465,6 +514,8 @@
             )
 
     arrive("wide", "far")
+    hear(0)
+    tell(1)
     for oz in (0, -1, 1):
         for oy in (0, -1, 1):
             if (oz, oy) == (0, 0):
@@ -491,35 +542,41 @@
     lane_iota = lax.broadcasted_iota(jnp.int32, (8, LANES), 1)
 
     def moduli_body(p):
-        plane = slab_at * PLANES + p.index()
+        plane = slab_at * PLANES + place(p, 0)
         plane_ok = (plane >= 0) & (plane < total_planes - 1)
+        stores = []
         for row in (-8, 0, 8):
             ip, ir = fine.at(p, row)
             rows = row_iota + (pencil_at * ROWS + row)
             keep = (rows >= 0) & (rows < total_rows - 1) & (lane_iota < LANES - 1) & plane_ok
             value = jnp.where(e_fine[ip, ir, :] > 0.5, 1.0, VOID_MODULUS)
-            e_fine[ip, ir, :] = jnp.where(keep, value, 0.0)
+            stores.append((e_fine, (ip, ir, ALL), jnp.where(keep, value, 0.0)))
+        return stores
 
     over((-6, 7), moduli_body)
 
     def fine_body(p):
-        plane = slab_at * PLANES + p.index()
+        plane = slab_at * PLANES + place(p, 0)
         inside = (plane > 0) & (plane < total_planes - 1)
+        stores = []
         for row in (-5, 3, 8):
             ip, ir = fine.at(p, row)
             total = fine.node_total(p, row)
             free = jnp.where((total > 0.9) & inside, 1.0, 0.0)
-            f_fine[ip, ir, :] = free
-            i_fine[0, ip, ir, :] = DAMPING / (free * total * fine.entries[0] + (1.0 - free))
+            weight = DAMPING / (free * total * fine.entries[0] + (1.0 - free))
+            stores += [(f_fine, (ip, ir, ALL), free), (i_fine, (0, ip, ir, ALL), weight)]
+        return stores
 
     over((-5, 7), fine_body)
 
     def first_update(p):
+        stores = []
         for row in (-4, 4, 8):
             ip, ir = fine.at(p, row)
             weight = i_fine[0, ip, ir, :] * f_fine[ip, ir, :]
             for c in COMPS:
-                fine.put_split(c, p, row, s0[c, ip, ir, :] * weight)
+                stores += fine.put_split(c, p, row, s0[c, ip, ir, :] * weight)
+        return stores
 
     over((-4, 7), first_update)
 
@@ -533,21 +590,25 @@
         return found
 
     def mid_moduli(p):
-        plane_ok = slab_at * (PLANES // 2) + p.index() < total_planes // 2 - 1
+        plane_ok = slab_at * (PLANES // 2) + place(p, 0) < total_planes // 2 - 1
+        stores = []
         for row in (-3, 0):
             ip, ir = mid.at(p, row)
             a, b, c, d = halves(e_fine, None, p, row)
             rows = row_iota + (pencil_at * (ROWS // 2) + row)
             keep = (rows < total_rows // 2 - 1) & plane_ok
-            e_mid[ip, ir, :] = jnp.where(keep, (a + b + c + d) * 0.25, 0.0)
+            stores.append((e_mid, (ip, ir, ALL), jnp.where(keep, (a + b + c + d) * 0.25, 0.0)))
+        return stores
 
     over((-3, 3), mid_moduli)
 
     def mid_free(p):
+        stores = []
         for row in (-2, 0):
             ip, ir = mid.at(p, row)
             a, b, c, d = halves(f_fine, None, p, row)
-            f_mid[ip, ir, :] = jnp.maximum(jnp.maximum(a, b), jnp.maximum(c, d))
+            stores.append((f_mid, (ip, ir, ALL), jnp.maximum(jnp.maximum(a, b), jnp.maximum(c, d))))
+        return stores
 
     over((-2, 3), mid_free)
     mid.set_diagonal((-2, 3), (-2, 0))
@@ -581,6 +642,7 @@
 
     def fine_step(rows, starting):
         def body(p):
+            stores = []
             for row in rows:
                 ip, ir = fine.at(p, row)
                 free = f_fine[ip, ir, :]
@@ -589,20 +651,24 @@
                     remain = s0[c, ip, ir, :]
                     update = weight * remain
                     remain = remain - free * fine.applied(c, p, row) - (1.0 - free) * update
-                    s0[c, ip, ir, :] = remain
+                    stores.append((s0, (c, ip, ir, ALL), remain))
                     if starting:
-                        fine.put_split(c, p, row, free * (weight * remain))
+                        stores += fine.put_split(c, p, row, free * (weight * remain))
+            return stores
 
         return body
 
     def estimate_add(starting):
         def body(p):
+            stores = []
             for row in (0, 8):
                 ip, ir = fine.at(p, row)
                 weight = i_fine[0, ip, ir, :]
                 for c in COMPS:
                     update = weight * s0[c, ip, ir, :]
-                    e0[c, p.index(), pl.ds(row, 8), :] = update if starting else e0[c, p.index(), pl.ds(row, 8), :] + update
+                    own = (c, place(p, 0), pl.ds(row, 8), ALL)
+                    stores.append((e0, own, update if starting else e0[own] + update))
+            return stores
 
         over((0, 3), body)
 
@@ -616,15 +682,16 @@
         ip, ir = mid.at(p, -1)
         free = f_mid[ip, ir, :]
         masks = halves(f_fine, None, p, -1)
+        stores = []
         for c in COMPS:
             parts = halves(s0, c, p, -1)
             rhs = free * (
                 (parts[0] * masks[0] + parts[1] * masks[1]) + (parts[2] * masks[2] + parts[3] * masks[3])
             )
-            s1[c, ip, ir, :] = rhs
             update = mid.inverse_of(c, p, -1) * rhs
-            u1[c, ip, ir, :] = update
-            mid.put_split(c, p, -1, free * update)
+            stores += [(s1, (c, ip, ir, ALL), rhs), (u1, (c, ip, ir, ALL), update)]
+            stores += mid.put_split(c, p, -1, free * update)
+        return stores
 
     over((-1, 2), mid_first)
     mid.voxels((-1, 1), (-1,))
@@ -632,8 +699,11 @@
     def mid_remain(p):
         ip, ir = mid.at(p, 0)
         free = f_mid[ip, ir, :]
+        stores = []
         for c in COMPS:
-            s1[c, ip, ir, :] = s1[c, ip, ir, :] - free * mid.applied(c, p, 0) - (1.0 - free) * u1[c, ip, ir, :]
+            remain = s1[c, ip, ir, :] - free * mid.applied(c, p, 0) - (1.0 - free) * u1[c, ip, ir, :]
+            stores.append((s1, (c, ip, ir, ALL), remain))
+        return stores
 
     over((0, 1), mid_remain)
 
@@ -659,6 +729,8 @@
                     at += count
     start("mid")
 
+    hear(1)
+    tell(2)
     arrive("dir")
     arrive("fixlow")
     def direction_rows(plane, first, count, c, value):
@@ -683,12 +755,15 @@
     fine.voxels((-1, 3), (-1, 7))
 
     def old_image(p):
+        stores = []
         for row in (0, 4):
             ip, ir = fine.at(p, row)
             free = f_fine[ip, ir, :]
             for c in COMPS:
-                value = dirn[c, p.index(), pl.ds(row, 8), :]
-                old[c, p.index(), pl.ds(row, 8), :] = free * fine.applied(c, p, row) + (1.0 - free) * value
+                value = dirn[c, place(p, 0), pl.ds(row, 8), :]
+                image = free * fine.applied(c, p, row) + (1.0 - free) * value
+                stores.append((old, (c, place(p, 0), pl.ds(row, 8), ALL), image))
+        return stores
 
     over((0, 3), old_image)
 
@@ -704,27 +779,33 @@
     low_window("fixlow", (e_low, f_low, m_low))
 
     def low_inverse(p):
+        stores = []
         for row in (-4, 4):
             ip, ir = low.at(p, row)
             free = f_low[ip, ir, :]
             total = m_low[ip, ir, :]
             for n, entry in enumerate(low.entries):
-                i_low[n, ip, ir, :] = DAMPING / (free * total * entry + (1.0 - free))
+                stores.append((i_low, (n, ip, ir, ALL), DAMPING / (free * total * entry + (1.0 - free))))
+        return stores
 
     over((-3, 3), low_inverse)
 
     arrive("low")
+    hear(2)
+    tell(3)
     low_window("low", [s2.at[c] for c in COMPS])
 
     def low_split(planes, rows):
         def body(p):
+            stores = []
             for row in rows:
                 ip, ir = low.at(p, row)
                 free = f_low[ip, ir, :]
                 for c in COMPS:
-                    low.put_split(c, p, row, free * (low.inverse_of(c, p, row) * s2[c, ip, ir, :]))
-
-        over(planes, body)
+                    stores += low.put_split(c, p, row, free * (low.inverse_of(c, p, row) * s2[c, ip, ir, :]))
+            return stores
+
+        over(planes, body, 7)
 
     ip, ir = low.at(0, 0)
     bottom = [low.inverse_of(c, 0, 0) * s2[c, ip, ir, :] for c in COMPS]
@@ -736,15 +817,17 @@
             row = -depth
             ip, ir = low.at(p, row)
             free = f_low[ip, ir, :]
+            stores = []
             for c in COMPS:
                 remain = s2[c, ip, ir, :]
                 update = low.inverse_of(c, p, row) * remain
                 remain = remain - free * low.applied(c, p, row) - (1.0 - free) * update
-                s2[c, ip, ir, :] = remain
+                stores.append((s2, (c, ip, ir, ALL), remain))
                 if depth:
-                    low.put_split(c, p, row, free * (low.inverse_of(c, p, row) * remain))
-
-        over((-depth, depth), low_step)
+                    stores += low.put_split(c, p, row, free * (low.inverse_of(c, p, row) * remain))
+            return stores
+
+        over((-depth, depth), low_step, 5)
         ip, ir = low.at(0, 0)
         for c in COMPS:
             bottom[c] = bottom[c] + low.inverse_of(c, 0, 0) * s2[c, ip, ir, :]
@@ -778,6 +861,10 @@
                         ref[c, p + 2 * oz + MID_O[0], pl.ds(first + MID_O[1], count), :] = inbox[pl.ds(at, count), :]
                         at += count
     arrive("lift")
+    for stage in range(3, STAGES):
+        if stage > 3:
+            tell(stage)
+        hear(stage)
     for oz in (0, -1, 1, -2, 2):
         for oy in (0, -1, 1):
             if (oz, oy) == (0, 0):
@@ -792,25 +879,31 @@
                     at += count
 
     def lift_split(p):
+        stores = []
         for row in (-3, 5):
             ip, ir = mid.at(p, row)
             for c in COMPS:
-                mid.put_split(c, p, row, c1[c, ip, ir, :])
+                stores += mid.put_split(c, p, row, c1[c, ip, ir, :])
+        return stores
 
     over((-3, 4), lift_split)
     mid.voxels((-3, 3), (-3, 5))
 
     def mid_second(p):
+        stores = []
         for row in (-2, 6):
             ip, ir = mid.at(p, row)
             free = f_mid[ip, ir, :]
             for c in COMPS:
                 remain = s1[c, ip, ir, :] - free * mid.applied(c, p, row)
-                u1[c, ip, ir, :] = u1[c, ip, ir, :] + c1[c, ip, ir, :] + mid.inverse_of(c, p, row) * remain
+                here = (c, ip, ir, ALL)
+                stores.append((u1, here, u1[here] + c1[here] + mid.inverse_of(c, p, row) * remain))
+        return stores
 
     over((-2, 3), mid_second)
 
     def lift_fine(p):
+        stores = []
         for row in (-2, 0):
             ip, ir = mid.at(p, row)
             for c in COMPS:
@@ -818,40 +911,46 @@
                 for dp in range(2):
                     for dr in range(2):
                         out = pl.ds(2 * row + dr + FINE_O[1], 8, stride=2)
-                        x_fine[2 * c, place(twice(p, dp), FINE_O[0]), out, :] = value
+                        stores.append((x_fine, (2 * c, place(twice(p, dp), FINE_O[0]), out, ALL), value))
+        return stores
 
     over((-2, 3), lift_fine)
 
     def lift_parts(p):
+        stores = []
         for row in (-4, 4, 12):
             ip, ir = fine.at(p, row)
             free = f_fine[ip, ir, :]
             for c in COMPS:
-                fine.put_split(c, p, row, free * x_fine[2 * c, ip, ir, :])
+                stores += fine.put_split(c, p, row, free * x_fine[2 * c, ip, ir, :])
+        return stores
 
     def lift_own(p):
-        for row in (0, 4):
+        stores = []
+        for row in (0, 8):
             ip, ir = fine.at(p, row)
             free = f_fine[ip, ir, :]
             for c in COMPS:
                 part = free * x_fine[2 * c, ip, ir, :]
-                if row:
-                    part = jnp.where(row_iota >= 4, part, 0.0)
-                e0[c, p.index(), pl.ds(row, 8), :] = e0[c, p.index(), pl.ds(row, 8), :] + part
+                own = (c, place(p, 0), pl.ds(row, 8), ALL)
+                stores.append((e0, own, e0[own] + part))
+        return stores
 
     over((0, 3), lift_own)
     over((-4, 7), lift_parts)
     fine.voxels((-3, 5), (-3, 5, 13))
 
     def lift_step(p):
+        stores = []
         for row in (-2, 6):
             ip, ir = fine.at(p, row)
             free = f_fine[ip, ir, :]
             weight = i_fine[0, ip, ir, :]
             for c in COMPS:
                 remain = s0[c, ip, ir, :] - free * fine.applied(c, p, row)
-                s0[c, ip, ir, :] = remain
-                fine.put_split(c, p, row, free * (weight * remain))
+                stores.append((s0, (c, ip, ir, ALL), remain))
+                stores += fine.put_split(c, p, row, free * (weight * remain))
+        return stores
 
     over((-2, 5), lift_step)
     estimate_add(False)
@@ -915,18 +1014,9 @@
                 new = r - s0[c, p + FINE_O[0], pl.ds(first + FINE_O[1], count), :]
                 nd = z + beta * d
                 image = new + beta * o
-                dir_in[c, there_rows, :] = nd
-                sol_in[c, there_rows, :] = sol_in[c, there_rows, :] + step * nd
-                res_in[c, there_rows, :] = r - step * image
-    stores = [
-        pltpu.make_async_copy(source, target, local_sem.at[n])
-        for n, (source, target) in enumerate(
-            ((dir_in, next_direction_ref), (sol_in, next_solution_ref), (res_in, next_residual_ref))
-        )
-    ]
-    for store in stores:
-        store.start()
-
+                next_direction_ref[c, there_rows, :] = nd
+                next_solution_ref[c, there_rows, :] = sol_in[c, there_rows, :] + step * nd
+                next_residual_ref[c, there_rows, :] = r - step * image
     for number, (name, oz, oy, key, rows) in enumerate(all_messages):
 
         @pl.when(there(-oz, -oy))
@@ -935,8 +1025,6 @@
 
     lax.fori_loop(1, slab_count, lambda k, _: (slab_copy(k).wait_send(), 0)[1], 0)
     lax.fori_loop(1, pencil_count, lambda k, _: (pencil_copy(k).wait_send(), 0)[1], 0)
-    for store in stores:
-        store.wait()
 
 
 def per_device(slab_count, pencil_count, solution, residual, direction, material, fixed):
@@ -960,7 +1048,7 @@
         functools.partial(kernel, slab_count, pencil_count),
         out_shape=(out, out, out),
         in_specs=[hbm] * 4,
-        out_specs=(hbm, hbm, hbm),
+        out_specs=(pl.BlockSpec(memory_space=pltpu.VMEM),) * 3,
         scratch_shapes=[
             vmem(*flat),
             vmem(*flat),
@@ -1002,6 +1090,7 @@
             pltpu.SemaphoreType.DMA((count,)),
             pltpu.SemaphoreType.DMA((2, max(slab_count, pencil_count))),
             pltpu.SemaphoreType.DMA((2, max(slab_count, pencil_count))),
+            pltpu.SemaphoreType.REGULAR((2, STAGES, 2)),
         ],
         compiler_params=pltpu.CompilerParams(collective_id=0, has_side_effects=True),
     )(*(inward(field) for field in (solution, residual, direction, material)))

time: 103 us -> 87.4 us (0.85)
  Pallas kernels: 99.1 us -> 82.8 us
    pallas_call x1, Pallas kernels: 99.1 us -> 82.8 us  [per_device(): pl.pallas_call(functools.partial(kernel, slab_count, pencil_count), out_s...]
where the time goes in v2:
time: 87.4 us; the launch traced here: 86.6 us
  Pallas kernels  82.8 us (95%)
  local copies, waits for them, and re-layouts  3.1 us (4%)
    pallas_call x1, Pallas kernels, per_device(): pl.pallas_call(functools.partial(kernel, slab_count, pencil_count), out_s...  82.8 us
    unnamed x7, local copies, waits for them, and re-layouts  3.1 us

profile of v2, /device:TPU:80, one launch (start us, length us, event | category | flops | bytes accessed | tf_op | source)
XLA Modules:
  0.0 86.6 jit_solution(10194671880156596446)
XLA Ops:
  0.6 82.8 %shard_map.67 = (f32[3,48,128]{2,1,0:T(8,128)}, f32[3,48,128]{2,1,0:T(8,128)}, f32[3,48,128]{2,1,0:T(8,128)}) custom-call(f32[3,48,128]{2,1,0:T(8,128)} %bitcast.24, f32[3,48,128]{2,1,0:T(8,128)} %bitcast.25, f32[3,48,128]{2,1,0:T(8,128)} %bitcast.26, s32[48,128]{1,0:T(8,128)} %bitcast.27), custom_call_target="tpu_custom_call" | custom-call | tf_op jit(solution)/shard_map/pallas_call | solution.py:1047
  83.5 0.0 copy-start.1
  83.5 1.6 %copy.10 = f32[3,4,12,128]{3,1,2,0:T(4,128)} copy(f32[3,4,12,128]{3,1,2,0:T(4,128)} %bitcast.23) | data formatting | bytes 147456
  85.0 0.0 copy-done.1
  85.0 0.0 copy-start
  85.0 0.6 copy.11
  85.7 0.3 copy-done
  85.9 0.6 copy.12
Async XLA Ops:
  83.5 1.6 %copy-start.1 = (f32[3,48,128]{2,1,0:T(8,128)S(1)}, f32[3,48,128]{2,1,0:T(8,128)}, u32[]{:S(2)}) copy-start(f32[3,48,128]{2,1,0:T(8,128)} %get-tuple-element.7) | copy-start | bytes 221188
  85.0 0.9 %copy-start = (f32[3,48,128]{2,1,0:T(8,128)S(1)}, f32[3,48,128]{2,1,0:T(8,128)}, u32[]{:S(2)}) copy-start(f32[3,48,128]{2,1,0:T(8,128)} %get-tuple-element.8) | copy-start | bytes 221188

commit v3 on v2

--- a/solution.py
+++ b/solution.py
@@ -19,7 +19,7 @@
 MESH = pl.DeviceIdType.MESH
 
 PLANES, ROWS = 4, 12
-REACH, STAGES = 3, 6
+REACH, STAGES = 2, 6
 FINE_O, FINE_S = (6, 8), (14, 32)
 MID_O, MID_S = (3, 4), (8, 24)
 LOW_O, LOW_S = (3, 4), (7, 24)
@@ -226,7 +226,9 @@
                 return upper, keep
 
             zero = [jnp.zeros((8, LANES), jnp.float32)] * 12
-            lax.fori_loop(0, planes[1] + 1 - planes[0], body, (pieces(planes[0], row), zero))
+            carry = (pieces(planes[0], row), zero)
+            for count in range(planes[1] + 1 - planes[0]):
+                carry = body(count, carry)
 
     def applied(self, c, plane, row):
         parts = []
@@ -237,6 +239,9 @@
             p, r = self.at(plane, row - 1)
             parts.append(here + self.sums[k + 1, p, r, :])
         return (parts[0] - parts[1]) + pltpu.roll(parts[0] + parts[1], 1, 1)
+
+
+NAMES = ("wide", "far", "dir", "fixlow", "low", "mid", "lift")
 
 
 def messages():
@@ -255,11 +260,11 @@
     for oz in (0, -1, 1, -2, 2, -3, 3):
         for oy in (0, -1, 1):
             if (oz, oy) != (0, 0):
-                found.append(("fixlow", oz, oy, ("fixlow",), 16))
+                found.append(("fixlow", oz, oy, ("fixlow",), 9))
     for oz in (0, -1, 1, -2, 2, -3, 3):
         for oy in (0, -1, 1):
             if (oz, oy) != (0, 0):
-                found.append(("low", oz, oy, ("low",), 16))
+                found.append(("low", oz, oy, ("low",), 9))
     for oz in (0, -1, 1):
         for oy in (0, -1, 1):
             if (oz, oy) != (0, 0):
@@ -267,9 +272,10 @@
     for oz in (0, -1, 1, -2, 2):
         for oy in (0, -1, 1):
             if (oz, oy) != (0, 0):
-                each = 16 if oy else 24
+                each = 9 if oy else 18
                 part = {-2: 1, 2: 0}.get(oz)
                 found.append(("lift", oz, oy, ("lift", oy, part), each if part is not None else 2 * each))
+    found.sort(key=lambda m: (NAMES.index(m[0]), -abs(m[1]) - 2 * abs(m[2])))
     return found
 
 
@@ -277,17 +283,17 @@
     sends, receives = {}, {}
     at_send = at_receive = 0
     for oy in (0, -1, 1):
-        each = 16 if oy else 24
+        each = 9 if oy else 18
         sends[("lift", oy, None)] = at_send
         sends[("lift", oy, 0)] = at_send
         sends[("lift", oy, 1)] = at_send + each
-        at_send += 2 * each
+        at_send += -(-2 * each // 8) * 8
     for name, oz, oy, key, rows in messages():
         if key not in sends:
             sends[key] = at_send
-            at_send += rows
+            at_send += -(-rows // 8) * 8
         receives[(name, oz, oy)] = at_receive
-        at_receive += rows
+        at_receive += -(-rows // 8) * 8
     return sends, at_send, receives, at_receive
 
 
@@ -453,8 +459,23 @@
                 def _(number=number, oz=oz, oy=oy, key=key, rows=rows):
                     copy_of(number, oz, oy, key, rows).wait_recv()
 
-    def take(name, oz, oy):
-        return receives[(name, oz, oy)]
+    def arrivals(*names):
+        for number, (name, oz, oy, key, rows) in reversed(list(enumerate(all_messages))):
+            if name in names:
+
+                @pl.when(there(oz, oy))
+                def _(number=number, oz=oz, oy=oy, key=key, rows=rows):
+                    copy_of(number, oz, oy, key, rows).wait_recv()
+
+                yield oz, oy, receives[(name, oz, oy)]
+
+    def left(*names):
+        for number, (name, oz, oy, key, rows) in enumerate(all_messages):
+            if name in names:
+
+                @pl.when(there(-oz, -oy))
+                def _(number=number, oz=oz, oy=oy, key=key, rows=rows):
+                    copy_of(number, oz, oy, key, rows).wait_send()
 
     def strided(p, first, count):
         return pl.ds(p + PLANES * first, count, stride=PLANES)
@@ -487,7 +508,12 @@
             outbox[pl.ds(at, count), :] = (mat[strided(p, first, count), :] == 1).astype(jnp.float32)
             at += count
 
+    pl.semaphore_wait(barrier, greeted)
+    start("wide", "far")
+    tell(0)
+
     loads[2].wait()
+    loads[3].wait()
     planes_first(dir_in, dirn)
     for name, oz, oy, key, rows in all_messages:
         if name == "dir":
@@ -498,11 +524,7 @@
                 for p in planes:
                     outbox[pl.ds(at, count), :] = dirn[c, p, pl.ds(first, count), :]
                     at += count
-
-    pl.semaphore_wait(barrier, greeted)
-    start("wide", "far")
     start("dir")
-    tell(0)
 
     for c in COMPS:
         for p in range(PLANES):
@@ -513,25 +535,19 @@
                 jnp.float32
             )
 
-    arrive("wide", "far")
+    for oz, oy, at in arrivals("wide"):
+        first, count = {0: (0, 12), -1: (-4, 4), 1: (12, 4)}[oy]
+        for c in COMPS:
+            for p in range(PLANES):
+                s0[c, p + oz * PLANES + FINE_O[0], pl.ds(first + FINE_O[1], count), :] = inbox[pl.ds(at, count), :]
+                at += count
+        first, count = {0: (0, 12), -1: (-6, 6), 1: (12, 4)}[oy]
+        for p in range(PLANES):
+            e_fine[p + oz * PLANES + FINE_O[0], pl.ds(first + FINE_O[1], count), :] = inbox[pl.ds(at, count), :]
+            at += count
     hear(0)
     tell(1)
-    for oz in (0, -1, 1):
-        for oy in (0, -1, 1):
-            if (oz, oy) == (0, 0):
-                continue
-            at = receives[("wide", oz, oy)]
-            first, count = {0: (0, 12), -1: (-4, 4), 1: (12, 4)}[oy]
-            for c in COMPS:
-                for p in range(PLANES):
-                    s0[c, p + oz * PLANES + FINE_O[0], pl.ds(first + FINE_O[1], count), :] = inbox[pl.ds(at, count), :]
-                    at += count
-            first, count = {0: (0, 12), -1: (-6, 6), 1: (12, 4)}[oy]
-            for p in range(PLANES):
-                e_fine[p + oz * PLANES + FINE_O[0], pl.ds(first + FINE_O[1], count), :] = inbox[pl.ds(at, count), :]
-                at += count
-    for oy in (0, -1, 1):
-        at = receives[("far", -2, oy)]
+    for _, oy, at in arrivals("far"):
         first, count = {0: (0, 12), -1: (-6, 6), 1: (12, 4)}[oy]
         for p in (-6, -5):
             e_fine[p + FINE_O[0], pl.ds(first + FINE_O[1], count), :] = inbox[pl.ds(at, count), :]
@@ -732,7 +748,6 @@
     hear(1)
     tell(2)
     arrive("dir")
-    arrive("fixlow")
     def direction_rows(plane, first, count, c, value):
         ip, ir = plane + FINE_O[0], pl.ds(first + FINE_O[1], count)
         value = value * f_fine[ip, ir, :]
@@ -768,13 +783,9 @@
     over((0, 3), old_image)
 
     def low_window(name, refs):
-        for oz in (0, -1, 1, -2, 2, -3, 3):
-            for oy in (0, -1, 1):
-                if (oz, oy) == (0, 0):
-                    continue
-                at = receives[(name, oz, oy)]
-                for n, ref in enumerate(refs):
-                    ref[oz + LOW_O[0], pl.ds(3 * oy + LOW_O[1], 3), :] = inbox[pl.ds(at + 3 * n, 3), :]
+        for oz, oy, at in arrivals(name):
+            for n, ref in enumerate(refs):
+                ref[oz + LOW_O[0], pl.ds(3 * oy + LOW_O[1], 3), :] = inbox[pl.ds(at + 3 * n, 3), :]
 
     low_window("fixlow", (e_low, f_low, m_low))
 
@@ -790,10 +801,9 @@
 
     over((-3, 3), low_inverse)
 
-    arrive("low")
+    low_window("low", [s2.at[c] for c in COMPS])
     hear(2)
     tell(3)
-    low_window("low", [s2.at[c] for c in COMPS])
 
     def low_split(planes, rows):
         def body(p):
@@ -848,35 +858,22 @@
                 outbox[pl.ds(at, count), :] = c1[c, p + MID_O[0], pl.ds(first + MID_O[1], count), :]
                 at += count
     start("lift")
-    arrive("mid")
-    for oz in (0, -1, 1):
-        for oy in (0, -1, 1):
-            if (oz, oy) == (0, 0):
-                continue
-            at = receives[("mid", oz, oy)]
-            first, count = {0: (0, 6), -1: (-2, 2), 1: (6, 2)}[oy]
-            for ref in (s1, u1):
-                for c in COMPS:
-                    for p in range(2):
-                        ref[c, p + 2 * oz + MID_O[0], pl.ds(first + MID_O[1], count), :] = inbox[pl.ds(at, count), :]
-                        at += count
-    arrive("lift")
-    for stage in range(3, STAGES):
-        if stage > 3:
-            tell(stage)
-        hear(stage)
-    for oz in (0, -1, 1, -2, 2):
-        for oy in (0, -1, 1):
-            if (oz, oy) == (0, 0):
-                continue
-            base = receives[("lift", oz, oy)]
-            first, count = {0: (0, 6), -1: (-3, 3), 1: (6, 3)}[oy]
-            planes = {-2: (-3,), 2: (4,)}.get(oz, (2 * oz, 2 * oz + 1))
-            for n, p in enumerate(planes):
-                at = base + n * (16 if oy else 24)
-                for c in COMPS:
-                    c1[c, p + MID_O[0], pl.ds(first + MID_O[1], count), :] = inbox[pl.ds(at, count), :]
+    for oz, oy, at in arrivals("mid"):
+        first, count = {0: (0, 6), -1: (-2, 2), 1: (6, 2)}[oy]
+        for ref in (s1, u1):
+            for c in COMPS:
+                for p in range(2):
+                    ref[c, p + 2 * oz + MID_O[0], pl.ds(first + MID_O[1], count), :] = inbox[pl.ds(at, count), :]
                     at += count
+    left("wide", "far", "dir", "fixlow", "low", "mid")
+    for oz, oy, base in arrivals("lift"):
+        first, count = {0: (0, 6), -1: (-3, 3), 1: (6, 3)}[oy]
+        planes = {-2: (-3,), 2: (4,)}.get(oz, (2 * oz, 2 * oz + 1))
+        for n, p in enumerate(planes):
+            at = base + n * (9 if oy else 18)
+            for c in COMPS:
+                c1[c, p + MID_O[0], pl.ds(first + MID_O[1], count), :] = inbox[pl.ds(at, count), :]
+                at += count
 
     def lift_split(p):
         stores = []
@@ -977,7 +974,7 @@
     for n, total in enumerate(totals):
         part_out[pl.ds(n, 1), :] = jnp.sum(total, axis=0, keepdims=True)
 
-    def share(axis, at, count, source, target, which):
+    def share(axis, at, count, source, target, which, meanwhile):
         def copy(k):
             return pltpu.make_async_remote_copy(
                 src_ref=source,
@@ -988,23 +985,39 @@
                 device_id_type=MESH,
             )
 
-        lax.fori_loop(1, count, lambda k, _: (copy(k).start(), 0)[1], 0)
-        lax.fori_loop(1, count, lambda k, _: (copy(k).wait_recv(), 0)[1], 0)
-        total = source[...]
-        total = lax.fori_loop(1, count, lambda k, t: t + target[k], total)
-        return total, copy
-
-    line, slab_copy = share("slab", slab_at, slab_count, part_out, slab_in, 0)
+        for k in order(count):
+            copy(k).start()
+        meanwhile()
+        for k in range(1, count):
+            copy(k).wait_recv()
+        parts = [source[...]] + [target[k] for k in range(1, count)]
+        while len(parts) > 1:
+            parts = [a + b for a, b in zip(parts[::2], parts[1::2])] + parts[len(parts) // 2 * 2 :]
+        return parts[0], copy
+
+    def order(count):
+        return sorted(range(1, count), key=lambda k: -min(k, count - k))
+
+    def settle():
+        left("lift")
+        for stage in range(3, STAGES):
+            if stage > 3:
+                tell(stage)
+            hear(stage)
+
+    def settle_slab():
+        for k in range(1, slab_count):
+            slab_copy(k).wait_send()
+
+    line, slab_copy = share("slab", slab_at, slab_count, part_out, slab_in, 0, settle)
     line_out[...] = line
-    whole, pencil_copy = share("pencil", pencil_at, pencil_count, line_out, pencil_in, 1)
+    whole, pencil_copy = share("pencil", pencil_at, pencil_count, line_out, pencil_in, 1, settle_slab)
     summed = jnp.sum(whole, axis=1, keepdims=True)
     t = [summed[n : n + 1, :] for n in range(5)]
     beta = -t[0] / t[1]
     along = t[3] + beta * t[4]
     curvature = t[2] + 2.0 * beta * t[0] + beta * beta * t[1]
     step = along / curvature
-
-    loads[3].wait()
 
     for c in COMPS:
         for p in range(PLANES):
@@ -1017,14 +1030,8 @@
                 next_direction_ref[c, there_rows, :] = nd
                 next_solution_ref[c, there_rows, :] = sol_in[c, there_rows, :] + step * nd
                 next_residual_ref[c, there_rows, :] = r - step * image
-    for number, (name, oz, oy, key, rows) in enumerate(all_messages):
-
-        @pl.when(there(-oz, -oy))
-        def _(number=number, oz=oz, oy=oy, key=key, rows=rows):
-            copy_of(number, oz, oy, key, rows).wait_send()
-
-    lax.fori_loop(1, slab_count, lambda k, _: (slab_copy(k).wait_send(), 0)[1], 0)
-    lax.fori_loop(1, pencil_count, lambda k, _: (pencil_copy(k).wait_send(), 0)[1], 0)
+    for k in range(1, pencil_count):
+        pencil_copy(k).wait_send()
 
 
 def per_device(slab_count, pencil_count, solution, residual, direction, material, fixed):
@@ -1092,8 +1099,8 @@
             pltpu.SemaphoreType.DMA((2, max(slab_count, pencil_count))),
             pltpu.SemaphoreType.REGULAR((2, STAGES, 2)),
         ],
-        compiler_params=pltpu.CompilerParams(collective_id=0, has_side_effects=True),
-    )(*(inward(field) for field in (solution, residual, direction, material)))
+        compiler_params=pltpu.CompilerParams(collective_id=0, has_side_effects=True, vmem_limit_bytes=24 * 1024 * 1024),
+    )(*(pltpu.with_memory_space_constraint(inward(field), pltpu.HBM) for field in (solution, residual, direction, material)))
     return tuple(outward(field) for field in results)
 
 

time: 87.4 us -> 83.5 us (0.955)
  Pallas kernels: 82.8 us -> 80 us
  local copies, waits for them, and re-layouts: 3.1 us -> 1.9 us
    pallas_call x1, Pallas kernels: 82.8 us -> 80 us  [per_device(): pl.pallas_call(functools.partial(kernel, slab_count, pencil_count), out_s...]
    unnamed x7 -> x3, local copies, waits for them, and re-layouts: 3.1 us -> 1.9 us
where the time goes in v3:
time: 83.5 us; the launch traced here: 82.6 us
  Pallas kernels  80 us (96%)
  local copies, waits for them, and re-layouts  1.9 us (2%)
    pallas_call x1, Pallas kernels, per_device(): pl.pallas_call(functools.partial(kernel, slab_count, pencil_count), out_s...  80 us
    unnamed x3, local copies, waits for them, and re-layouts  1.9 us

profile of v3, /device:TPU:80, one launch (start us, length us, event | category | flops | bytes accessed | tf_op | source)
XLA Modules:
  0.0 82.6 jit_solution(1694453492440749425)
XLA Ops:
  0.6 80.0 %shard_map.67 = (f32[3,48,128]{2,1,0:T(8,128)S(1)}, f32[3,48,128]{2,1,0:T(8,128)S(1)}, f32[3,48,128]{2,1,0:T(8,128)S(1)}) custom-call(f32[3,48,128]{2,1,0:T(8,128)} %bitcast.24, f32[3,48,128]{2,1,0:T(8,128)} %bitcast.25, f32[3,48,128]{2,1,0:T(8,128)} %bitcast.26, s32[48,128]{1,0:T(8,128)} %bitcast.27), custom_call_target="tpu_custom_call" | custom-call | tf_op jit(solution)/shard_map/pallas_call | solution.py:1054
  80.7 0.6 copy.10
  81.3 0.6 copy.11
  81.9 0.6 copy.12

commit v4 on v3

--- a/solution.py
+++ b/solution.py
@@ -338,9 +338,7 @@
     b_low,
     outbox,
     inbox,
-    part_out,
     slab_in,
-    line_out,
     pencil_in,
     local_sem,
     send_sem,
@@ -971,14 +969,21 @@
         return tuple(totals)
 
     totals = lax.fori_loop(0, PLANES, dots, (jnp.zeros((8, LANES), jnp.float32),) * 5)
-    for n, total in enumerate(totals):
-        part_out[pl.ds(n, 1), :] = jnp.sum(total, axis=0, keepdims=True)
-
-    def share(axis, at, count, source, target, which, meanwhile):
+    width = LANES // 8
+    owner = lane_iota // width == row_iota
+    rows = [jnp.sum(total, axis=0, keepdims=True) for total in totals]
+    folded = jnp.concatenate(rows + [jnp.zeros((3, LANES), jnp.float32)], axis=0)
+    shift = LANES // 2
+    while shift >= width:
+        folded = folded + pltpu.roll(folded, shift, 1)
+        shift //= 2
+    slab_in[pl.ds(0, 1), :] = jnp.sum(jnp.where(owner, folded, 0.0), axis=0, keepdims=True)
+
+    def share(axis, at, count, target, which, meanwhile):
         def copy(k):
             return pltpu.make_async_remote_copy(
-                src_ref=source,
-                dst_ref=target.at[k],
+                src_ref=target.at[pl.ds(0, 1)],
+                dst_ref=target.at[pl.ds(k, 1)],
                 send_sem=sum_send.at[which, k],
                 recv_sem=sum_recv.at[which, k],
                 device_id={axis: lax.rem(at + k, count)},
@@ -990,10 +995,7 @@
         meanwhile()
         for k in range(1, count):
             copy(k).wait_recv()
-        parts = [source[...]] + [target[k] for k in range(1, count)]
-        while len(parts) > 1:
-            parts = [a + b for a, b in zip(parts[::2], parts[1::2])] + parts[len(parts) // 2 * 2 :]
-        return parts[0], copy
+        return jnp.sum(target[...], axis=0, keepdims=True), copy
 
     def order(count):
         return sorted(range(1, count), key=lambda k: -min(k, count - k))
@@ -1009,10 +1011,10 @@
         for k in range(1, slab_count):
             slab_copy(k).wait_send()
 
-    line, slab_copy = share("slab", slab_at, slab_count, part_out, slab_in, 0, settle)
-    line_out[...] = line
-    whole, pencil_copy = share("pencil", pencil_at, pencil_count, line_out, pencil_in, 1, settle_slab)
-    summed = jnp.sum(whole, axis=1, keepdims=True)
+    line, slab_copy = share("slab", slab_at, slab_count, slab_in, 0, settle)
+    pencil_in[pl.ds(0, 1), :] = line
+    whole, pencil_copy = share("pencil", pencil_at, pencil_count, pencil_in, 1, settle_slab)
+    summed = jnp.sum(jnp.where(owner, jnp.broadcast_to(whole, (8, LANES)), 0.0), axis=1, keepdims=True)
     t = [summed[n : n + 1, :] for n in range(5)]
     beta = -t[0] / t[1]
     along = t[3] + beta * t[4]
@@ -1088,10 +1090,8 @@
             vmem(12, *window(LOW_S)),
             vmem(send_rows, LANES),
             vmem(receive_rows, LANES),
-            vmem(8, LANES),
-            vmem(slab_count, 8, LANES),
-            vmem(8, LANES),
-            vmem(pencil_count, 8, LANES),
+            vmem(slab_count, LANES),
+            vmem(pencil_count, LANES),
             pltpu.SemaphoreType.DMA((4,)),
             pltpu.SemaphoreType.DMA((count,)),
             pltpu.SemaphoreType.DMA((count,)),
@@ -1101,7 +1101,23 @@
         ],
         compiler_params=pltpu.CompilerParams(collective_id=0, has_side_effects=True, vmem_limit_bytes=24 * 1024 * 1024),
     )(*(pltpu.with_memory_space_constraint(inward(field), pltpu.HBM) for field in (solution, residual, direction, material)))
+    results = pl.pallas_call(
+        hand_over,
+        out_shape=(out, out, out),
+        in_specs=[pl.BlockSpec(memory_space=pltpu.VMEM)] * 3,
+        out_specs=(hbm, hbm, hbm),
+        scratch_shapes=[pltpu.SemaphoreType.DMA((3,))],
+        compiler_params=pltpu.CompilerParams(vmem_limit_bytes=24 * 1024 * 1024),
+    )(*results)
     return tuple(outward(field) for field in results)
+
+
+def hand_over(*refs):
+    copies = [pltpu.make_async_copy(refs[n], refs[3 + n], refs[6].at[n]) for n in range(3)]
+    for copy in copies:
+        copy.start()
+    for copy in copies:
+        copy.wait()
 
 
 def inward(field):

time: 83.5 us -> 80.8 us (0.968)
  local copies, waits for them, and re-layouts: 1.9 us -> 0 us
    unnamed x3 -> x0, local copies, waits for them, and re-layouts: 1.9 us -> none
where the time goes in v4:
time: 80.8 us; the launch traced here: 80.6 us
  Pallas kernels  80 us (99%)
    pallas_call x1, Pallas kernels, per_device(): pl.pallas_call(functools.partial(kernel, slab_count, pencil_count), out_s...  79.2 us

profile of v4, /device:TPU:80, one launch (start us, length us, event | category | flops | bytes accessed | tf_op | source)
XLA Modules:
  0.0 80.6 jit_solution(2844751435720473596)
XLA Ops:
  0.6 79.2 %shard_map.67 = (f32[3,48,128]{2,1,0:T(8,128)S(1)}, f32[3,48,128]{2,1,0:T(8,128)S(1)}, f32[3,48,128]{2,1,0:T(8,128)S(1)}) custom-call(f32[3,48,128]{2,1,0:T(8,128)} %bitcast.21, f32[3,48,128]{2,1,0:T(8,128)} %bitcast.22, f32[3,48,128]{2,1,0:T(8,128)} %bitcast.23, s32[48,128]{1,0:T(8,128)} %bitcast.24), custom_call_target="tpu_custom_call" | custom-call | tf_op jit(solution)/shard_map/pallas_call | solution.py:1056
  79.9 0.7 shard_map.68

commit v5 on v4

--- a/solution.py
+++ b/solution.py
@@ -522,7 +522,6 @@
                 for p in planes:
                     outbox[pl.ds(at, count), :] = dirn[c, p, pl.ds(first, count), :]
                     at += count
-    start("dir")
 
     for c in COMPS:
         for p in range(PLANES):
@@ -543,6 +542,7 @@
         for p in range(PLANES):
             e_fine[p + oz * PLANES + FINE_O[0], pl.ds(first + FINE_O[1], count), :] = inbox[pl.ds(at, count), :]
             at += count
+    start("dir")
     hear(0)
     tell(1)
     for _, oy, at in arrivals("far"):

time: 80.8 us -> 80.6 us (level)
  no operation moved by 1% of the time
where the time goes in v5:
time: 80.6 us; the launch traced here: 80.4 us
  Pallas kernels  79.8 us (99%)
    pallas_call x1, Pallas kernels, per_device(): pl.pallas_call(functools.partial(kernel, slab_count, pencil_count), out_s...  79.1 us

profile of v5, /device:TPU:80, one launch (start us, length us, event | category | flops | bytes accessed | tf_op | source)
XLA Modules:
  0.0 80.4 jit_solution(7976835930065652638)
XLA Ops:
  0.6 79.1 %shard_map.67 = (f32[3,48,128]{2,1,0:T(8,128)S(1)}, f32[3,48,128]{2,1,0:T(8,128)S(1)}, f32[3,48,128]{2,1,0:T(8,128)S(1)}) custom-call(f32[3,48,128]{2,1,0:T(8,128)} %bitcast.21, f32[3,48,128]{2,1,0:T(8,128)} %bitcast.22, f32[3,48,128]{2,1,0:T(8,128)} %bitcast.23, s32[48,128]{1,0:T(8,128)} %bitcast.24), custom_call_target="tpu_custom_call" | custom-call | tf_op jit(solution)/shard_map/pallas_call | solution.py:1056
  79.7 0.7 shard_map.68
